TPU v7x, 32 devices: a whole 2x2x4 slice. The times are simulated.
32 devices in a mesh: freq: 8 (over z, core), tm: 4 (over y, x).
Axes of the slice: x: 2, y: 2, z: 4, core: 2. Of those that a mesh axis runs over, the one named last changes fastest.
Arguments:
- band_state: float32 [2048, 4096], P('freq', 'tm'), may hold values from -2.5 to 2.5
- lower_rows: int32 [3, 2048], replicated, may hold values from 0 to 2047, as said below
- upper_rows: int32 [3, 2048], replicated, may hold values from 0 to 2047, as said below
- delays: int32 [3, 2048], replicated, may hold values from 0 to 1024, as said below
- counts: int32 [7], replicated, may hold values from 256 to 2048, as said below
Outputs:
- dedispersed: float32 [2048, 4096], P('freq', 'tm')
Inputs may be any that keep to these rules, and one draw needn't show every extreme that they name: `counts`: entry 8 - 8 / 2^k + b is the live row count of output sub-band b of iteration k; it lies between half and all of that sub-band's 2 * 2048 / 2^(3 - k) padded rows, and in every iteration some sub-band has all its rows live. With w = 2048 / 2^(3 - k), lower_rows[k, i] is a row of input sub-band 2 * floor(i / (2 * w)) whose position in that sub-band is below its live count (all w rows are live in iteration 0). With w = 2048 / 2^(3 - k), upper_rows[k, i] is a row of input sub-band 2 * floor(i / (2 * w)) + 1 whose position in that sub-band is below its live count (all w rows are live in iteration 0). delays[k, i] is at most 2048 / 2^(3 - k), and equals it at some row in every iteration.
All inputs are finite; a program needn't handle non-finite values.
Results may differ from a plain program's by a relative error of at most 0.0003.
Values sent between devices are 32-bit elements; how exact they have to be, the bound alone decides.
A program may use at most 64 MiB of HBM per device.

v0:
```python
import functools

import jax
import jax.numpy as jnp
from jax import lax
from jax.experimental import pallas as pl
from jax.experimental.pallas import tpu as pltpu
from jax.sharding import PartitionSpec as P

DMAX = 2048
ITERS = 3
LANES = 128
SUBLANES = 8
UNROLL = 16
CHUNKS_0 = 4
CHUNKS_1 = 8
CHUNKS_2 = 16


def shifted_2(block, axis, distance):
    devices = range(lax.axis_size(axis))
    route = [(i - distance, i) for i in devices if i - distance in devices]
    return lax.ppermute(block, axis, route)


def delay_columns(extended, shifts, widest):
    row_count = extended.shape[0]
    for bit_index in range(widest.bit_length()):
        stride = 1 << bit_index
        shifted = jnp.concatenate(
            [jnp.zeros((row_count, stride), extended.dtype), extended[:, :-stride]], axis=1
        )
        extended = jnp.where((shifts >> bit_index & 1)[:, None] == 1, shifted, extended)
    return extended


def live_mask(global_rows, counts, width_out, offset, bands_out):
    band_index = global_rows // width_out
    band_counts = counts[offset : offset + bands_out]
    matches = band_index[:, None] == jnp.arange(bands_out, dtype=jnp.int32)[None, :]
    live_count = jnp.sum(jnp.where(matches, band_counts[None, :], 0), axis=1)
    return global_rows % width_out < live_count


def per_device_general(band_state, lower_rows, upper_rows, delays, counts):
    row_count, samples = band_state.shape
    freq_index = lax.axis_index("freq")
    first_row = freq_index * row_count
    global_rows = first_row + jnp.arange(row_count, dtype=jnp.int32)
    current = band_state
    for iteration in range(ITERS):
        width_in = DMAX >> ITERS - iteration
        width_out = 2 * width_in
        bands_out = DMAX // width_out
        offset = 2**ITERS - 2 ** (ITERS - iteration)
        lower_source = lax.dynamic_slice_in_dim(lower_rows[iteration], first_row, row_count)
        upper_source = lax.dynamic_slice_in_dim(upper_rows[iteration], first_row, row_count)
        own_delays = lax.dynamic_slice_in_dim(delays[iteration], first_row, row_count)
        gathered = lax.all_gather(current, "freq", axis=0, tiled=True)
        lower_values = jnp.take(gathered, lower_source, axis=0)
        upper_values = jnp.take(gathered, upper_source, axis=0)
        rim_columns = shifted_2(upper_values[:, samples - width_in :], "tm", 1)
        extended = jnp.concatenate([rim_columns, upper_values], axis=1)
        delayed = delay_columns(extended, own_delays, width_in)[:, width_in:]
        live_rows = live_mask(global_rows, counts, width_out, offset, bands_out)
        current = jnp.where(live_rows[:, None], lower_values + delayed, jnp.zeros_like(delayed))
    return current


class Flow:
    def __init__(self, buffer, sems, first, chunk):
        self.buffer, self.sems, self.first, self.chunk = buffer, sems, first, chunk

    def copy(self, j, row, target, source_at, target_at, size):
        rows = pl.ds(row + j * self.chunk, self.chunk)
        return pltpu.make_async_remote_copy(
            src_ref=self.buffer.at[rows, pl.ds(source_at, size)],
            dst_ref=self.buffer.at[rows, pl.ds(target_at, size)],
            send_sem=self.sems.at[0, self.first + j],
            recv_sem=self.sems.at[1, self.first + j],
            device_id=target,
            device_id_type=pl.DeviceIdType.MESH,
        )


def kernel(tiles, tm_size, x_ref, lower, upper, delays, counts, out_ref, b0, b1, b2, final, s0, s1, s2):
    f, t = lax.axis_index("freq"), lax.axis_index("tm")
    c, z = lax.rem(f, 2), lax.div(f, 2)
    zb, half = lax.rem(z, 2), lax.div(z, 2)
    z_size = 2 ** (ITERS - 1)
    rows = x_ref.shape[0]
    at = lambda ff, tt: {"freq": ff, "tm": tt}
    partner = at(f + 1 - 2 * c, t)
    later = at(f, t + 1)
    pair = at(f + 2 - 4 * zb, t)
    inner = zb != half
    facing = at(f + 2 - 4 * half, t)
    outer = at(f - 2 + 4 * half, t)
    has_later, has_earlier = t < tm_size - 1, t > 0

    barrier = pltpu.get_barrier_semaphore()

    def greet(target):
        pl.semaphore_signal(barrier, inc=1, device_id=target, device_id_type=pl.DeviceIdType.MESH)

    greet(partner)
    for cond, target in (
        (z > 0, at(f - 2, t)),
        (z < z_size - 1, at(f + 2, t)),
        (has_earlier, at(f, t - 1)),
        (has_later, later),
    ):
        pl.when(cond)(functools.partial(greet, target))
    one = lambda cond: jnp.where(cond, 1, 0)
    pl.semaphore_wait(barrier, 1 + one(z > 0) + one(z < z_size - 1) + one(has_earlier) + one(has_later))

    lane = lax.broadcasted_iota(jnp.int32, (tiles, LANES), 1)

    def merge(k, source, first, position, start, count, store):
        width_in = DMAX >> ITERS - k
        rim = width_in // LANES
        width_out = 2 * width_in
        band = lax.div(first, width_out)
        limit = counts[2**ITERS - 2 ** (ITERS - k) + band]
        wrap = width_out - 1

        def body(step, carry):
            values = []
            for u in range(UNROLL):
                i = start + step * UNROLL + u
                g = first + i
                lo, up, d = lower[k, g] & wrap, upper[k, g] & wrap, delays[k, g]
                q, r = d >> 7, d & (LANES - 1)
                a = source[up, pl.ds(tiles - q, tiles), :]
                b = source[up, pl.ds(jnp.maximum(tiles - 1 - q, tiles - rim), tiles), :]
                a, b = pltpu.roll(a, r, 1), pltpu.roll(b, r, 1)
                total = source[lo, tiles:, :] + jnp.where(lane >= r, a, b)
                values.append((i, jnp.where(position + i < limit, total, jnp.zeros_like(total))))
            for i, value in values:
                store(i, value)
            return carry

        lax.fori_loop(0, count // UNROLL, body, 0)

    def when(cond, action):
        pl.when(cond)(action)

    rim0 = rows // LANES
    n0, chunk0 = CHUNKS_0, rows // CHUNKS_0
    own0, rim_out0, rim_in0 = [Flow(b0, s0, kind * n0, chunk0) for kind in range(3)]
    upper0 = rows
    tail0 = (2 * tiles - rim0, tiles - rim0, rim0)
    kept0 = (tiles - rim0, tiles - rim0, rim0)
    full0 = (tiles, tiles, tiles)

    def spread(first, count):
        def body(step, carry):
            r = first + step * SUBLANES
            for tile in range(tiles):
                b0[pl.ds(c * rows + r, SUBLANES), tiles + tile, :] = x_ref[
                    pl.ds(r, SUBLANES), pl.ds(tile * LANES, LANES)
                ]
            return carry

        lax.fori_loop(0, count // SUBLANES, body, 0)

    for j in range(n0):
        spread(j * chunk0, chunk0)
        when((c == 1) & has_later, rim_out0.copy(j, upper0, later, *tail0).start)
        own0.copy(j, c * rows, partner, *full0).start()

    @pl.when(t == 0)
    def _():
        for buffer in (b0, b1, b2):
            first = buffer.shape[0] // 2

            def clear(i, carry, buffer=buffer, first=first):
                for u in range(UNROLL):
                    buffer[first + i * UNROLL + u, :tiles, :] = jnp.zeros((tiles, LANES), jnp.float32)
                return carry

            lax.fori_loop(0, first // UNROLL, clear, 0)

    for j in range(n0):

        @pl.when((c == 1) & has_earlier)
        def _():
            rim_out0.copy(j, upper0, later, *tail0).wait_recv()
            rim_in0.copy(j, upper0, partner, *kept0).start()

    for j in range(n0):
        own0.copy(j, (1 - c) * rows, partner, *full0).wait_recv()
        when((c == 0) & has_earlier, rim_in0.copy(j, upper0, partner, *kept0).wait_recv)

    rim1 = 2 * rows // LANES
    n1, chunk1 = CHUNKS_1, rows // CHUNKS_1
    flows1 = [Flow(b1, s1, kind * n1, chunk1) for kind in range(5)]
    own1, pair1, pass1, rim_out1, rim_in1 = flows1
    mine1 = zb * 2 * rows + c * rows
    other1 = (1 - zb) * 2 * rows + c * rows
    upper1 = 2 * rows + c * rows
    wide = (tiles, tiles, tiles)
    tail1 = (2 * tiles - rim1, tiles - rim1, rim1)
    kept1 = (tiles - rim1, tiles - rim1, rim1)

    def store1(i, value):
        b1[mine1 + i, tiles:, :] = value

    for j in range(n1):
        merge(0, b0, f * rows, c * rows, j * chunk1, chunk1, store1)
        pair1.copy(j, mine1, pair, *wide).start()
        own1.copy(j, mine1, partner, *wide).start()
        when((zb == 1) & has_later, rim_out1.copy(j, upper1, later, *tail1).start)
    for j in range(n1):
        pair1.copy(j, other1, pair, *wide).wait_recv()
        when((zb == 0) & has_later, rim_out1.copy(j, upper1, later, *tail1).start)
        pass1.copy(j, other1, partner, *wide).start()

        @pl.when(has_earlier)
        def _():
            rim_out1.copy(j, upper1, later, *tail1).wait_recv()
            rim_in1.copy(j, upper1, partner, *kept1).start()

    across = (1 - 2 * c) * rows
    for j in range(n1):
        own1.copy(j, mine1 + across, partner, *wide).wait_recv()
        pass1.copy(j, other1 + across, partner, *wide).wait_recv()
        when(has_earlier, rim_in1.copy(j, upper1 + across, partner, *kept1).wait_recv)

    n2, chunk2 = CHUNKS_2, 2 * rows // CHUNKS_2
    flows2 = [Flow(b2, s2, kind * n2, chunk2) for kind in range(5)]
    own2, z2, pass2, rim_out2, rim_in2 = flows2
    mine2 = half * 4 * rows + c * 2 * rows
    other2 = (1 - half) * 4 * rows + c * 2 * rows
    upper2 = 4 * rows + c * 2 * rows
    tail2 = (tiles, 0, tiles)
    kept2 = (0, 0, tiles)

    def store2(i, value):
        b2[mine2 + i, tiles:, :] = value

    for j in range(n2):
        merge(1, b1, half * 4 * rows + c * 2 * rows, c * 2 * rows, j * chunk2, chunk2, store2)
        when(inner, z2.copy(j, mine2, facing, *wide).start)
        when((half == 1) & has_later, rim_out2.copy(j, upper2, later, *tail2).start)
        own2.copy(j, mine2, partner, *wide).start()
    for j in range(n2):
        z2.copy(j, other2, partner, *wide).wait_recv()
        when(
            inner,
            pltpu.make_async_remote_copy(
                src_ref=b2.at[pl.ds(other2 + j * chunk2, chunk2), pl.ds(tiles, tiles)],
                dst_ref=b2.at[pl.ds(other2 + j * chunk2, chunk2), pl.ds(tiles, tiles)],
                send_sem=s2.at[0, 5 * n2 + j],
                recv_sem=s2.at[1, n2 + j],
                device_id=outer,
                device_id_type=pl.DeviceIdType.MESH,
            ).start,
        )
        when((half == 0) & has_later, rim_out2.copy(j, upper2, later, *tail2).start)
        pass2.copy(j, other2, partner, *wide).start()

        @pl.when(has_earlier)
        def _():
            rim_out2.copy(j, upper2, later, *tail2).wait_recv()
            rim_in2.copy(j, upper2, partner, *kept2).start()

    across = (1 - 2 * c) * 2 * rows
    for j in range(n2):
        own2.copy(j, mine2 + across, partner, *wide).wait_recv()
        pass2.copy(j, other2 + across, partner, *wide).wait_recv()
        when(has_earlier, rim_in2.copy(j, upper2 + across, partner, *kept2).wait_recv)

    def store_out(i, value):
        final[i] = value

    merge(2, b2, f * rows, f * rows, 0, rows, store_out)

    def flatten(step, carry):
        r = step * SUBLANES
        for tile in range(tiles):
            out_ref[pl.ds(r, SUBLANES), pl.ds(tile * LANES, LANES)] = final[pl.ds(r, SUBLANES), tile, :]
        return carry

    lax.fori_loop(0, rows // SUBLANES, flatten, 0)

    for j in range(n0):
        own0.copy(j, c * rows, partner, *full0).wait_send()
        when((c == 1) & has_later, rim_out0.copy(j, upper0, later, *tail0).wait_send)
        when((c == 1) & has_earlier, rim_in0.copy(j, upper0, partner, *kept0).wait_send)
    for j in range(n1):
        pair1.copy(j, mine1, pair, *wide).wait_send()
        own1.copy(j, mine1, partner, *wide).wait_send()
        pass1.copy(j, other1, partner, *wide).wait_send()
        when(has_later, rim_out1.copy(j, upper1, later, *tail1).wait_send)
        when(has_earlier, rim_in1.copy(j, upper1, partner, *kept1).wait_send)
    for j in range(n2):
        own2.copy(j, mine2, partner, *wide).wait_send()
        pass2.copy(j, other2, partner, *wide).wait_send()
        when(has_later, rim_out2.copy(j, upper2, later, *tail2).wait_send)
        when(has_earlier, rim_in2.copy(j, upper2, partner, *kept2).wait_send)

        @pl.when(inner)
        def _():
            z2.copy(j, mine2, facing, *wide).wait_send()
            pltpu.make_async_remote_copy(
                src_ref=b2.at[pl.ds(other2 + j * chunk2, chunk2), pl.ds(tiles, tiles)],
                dst_ref=b2.at[pl.ds(other2 + j * chunk2, chunk2), pl.ds(tiles, tiles)],
                send_sem=s2.at[0, 5 * n2 + j],
                recv_sem=s2.at[1, n2 + j],
                device_id=outer,
                device_id_type=pl.DeviceIdType.MESH,
            ).wait_send()


def per_device_fused(tm_size, band_state, lower_rows, upper_rows, delays, counts):
    row_count, samples = band_state.shape
    tiles = samples // LANES
    dma = pltpu.SemaphoreType.DMA
    return pl.pallas_call(
        functools.partial(kernel, tiles, tm_size),
        out_shape=jax.ShapeDtypeStruct((row_count, samples), jnp.float32),
        in_specs=[pl.BlockSpec(memory_space=pltpu.VMEM)] + [pl.BlockSpec(memory_space=pltpu.SMEM)] * 4,
        out_specs=pl.BlockSpec(memory_space=pltpu.VMEM),
        scratch_shapes=[
            pltpu.VMEM((2 * row_count, 2 * tiles, LANES), jnp.float32),
            pltpu.VMEM((4 * row_count, 2 * tiles, LANES), jnp.float32),
            pltpu.VMEM((8 * row_count, 2 * tiles, LANES), jnp.float32),
            pltpu.VMEM((row_count, tiles, LANES), jnp.float32),
            dma((2, 3 * CHUNKS_0)),
            dma((2, 5 * CHUNKS_1)),
            dma((2, 6 * CHUNKS_2)),
        ],
        compiler_params=pltpu.CompilerParams(
            collective_id=0, has_side_effects=True, vmem_limit_bytes=60 * 2**20
        ),
    )(band_state, lower_rows, upper_rows, delays, counts)


def solution(mesh):
    if mesh.shape["freq"] == 2**ITERS:
        body = functools.partial(per_device_fused, mesh.shape["tm"])
    else:
        body = per_device_general
    return jax.shard_map(
        body,
        mesh=mesh,
        in_specs=(P("freq", "tm"), P(), P(), P(), P()),
        out_specs=P("freq", "tm"),
        check_vma=False,
    )
```

profile of v0, /device:TPU:7, one launch (start us, length us, event | category | flops | bytes accessed | tf_op | source)
XLA Modules:
  0.0 105.8 jit_solution(8646621816564815206)
XLA Ops:
  0.0 103.4 %shard_map.55 = f32[256,1024]{1,0:T(8,128)} custom-call(f32[256,1024]{1,0:T(8,128)} %x_ref.1, s32[3,2048]{1,0:T(4,128)} %lower.1, s32[3,2048]{1,0:T(4,128)} %upper.1, s32[3,2048]{1,0:T(4,128)} %delays.1, s32[7]{0:T(128)} %counts.1), custom_call_target="tpu_custom_call" | custom-call | tf_op jit(solution)/shard_map/pallas_call | solution.py:320
  103.5 2.3 %copy.7 = f32[256,1024]{1,0:T(8,128)} copy(f32[256,1024]{1,0:T(8,128)} %shard_map.55) | data formatting | bytes 2097152
where the time goes:
time: 106 us
  Pallas kernels  103 us (97%)
  local copies, waits for them, and re-layouts  2.31 us (2%)
    pallas_call x1, Pallas kernels, per_device_fused(): pl.pallas_call(functools.partial(kernel, tiles, tm_size), out_shape=jax.S...  103 us
    unnamed x1, local copies, waits for them, and re-layouts  2.31 us

commit v1 on v0

v1 whole, which is shorter than its diff:
```python
import functools

import jax
import jax.numpy as jnp
from jax import lax
from jax.experimental import pallas as pl
from jax.experimental.pallas import tpu as pltpu
from jax.sharding import PartitionSpec as P

DMAX = 2048
ITERS = 3
LANES = 128
SUBLANES = 8
UNROLL = 16
CHUNKS_0 = 4
CHUNK_ROWS = 16
HALO_LAG = 2
MERGE_LAG = 3
EDGE_LAG = 2


def shifted_2(block, axis, distance):
    devices = range(lax.axis_size(axis))
    route = [(i - distance, i) for i in devices if i - distance in devices]
    return lax.ppermute(block, axis, route)


def delay_columns(extended, shifts, widest):
    row_count = extended.shape[0]
    for bit_index in range(widest.bit_length()):
        stride = 1 << bit_index
        shifted = jnp.concatenate(
            [jnp.zeros((row_count, stride), extended.dtype), extended[:, :-stride]], axis=1
        )
        extended = jnp.where((shifts >> bit_index & 1)[:, None] == 1, shifted, extended)
    return extended


def live_mask(global_rows, counts, width_out, offset, bands_out):
    band_index = global_rows // width_out
    band_counts = counts[offset : offset + bands_out]
    matches = band_index[:, None] == jnp.arange(bands_out, dtype=jnp.int32)[None, :]
    live_count = jnp.sum(jnp.where(matches, band_counts[None, :], 0), axis=1)
    return global_rows % width_out < live_count


def per_device_general(band_state, lower_rows, upper_rows, delays, counts):
    row_count, samples = band_state.shape
    freq_index = lax.axis_index("freq")
    first_row = freq_index * row_count
    global_rows = first_row + jnp.arange(row_count, dtype=jnp.int32)
    current = band_state
    for iteration in range(ITERS):
        width_in = DMAX >> ITERS - iteration
        width_out = 2 * width_in
        bands_out = DMAX // width_out
        offset = 2**ITERS - 2 ** (ITERS - iteration)
        lower_source = lax.dynamic_slice_in_dim(lower_rows[iteration], first_row, row_count)
        upper_source = lax.dynamic_slice_in_dim(upper_rows[iteration], first_row, row_count)
        own_delays = lax.dynamic_slice_in_dim(delays[iteration], first_row, row_count)
        gathered = lax.all_gather(current, "freq", axis=0, tiled=True)
        lower_values = jnp.take(gathered, lower_source, axis=0)
        upper_values = jnp.take(gathered, upper_source, axis=0)
        rim_columns = shifted_2(upper_values[:, samples - width_in :], "tm", 1)
        extended = jnp.concatenate([rim_columns, upper_values], axis=1)
        delayed = delay_columns(extended, own_delays, width_in)[:, width_in:]
        live_rows = live_mask(global_rows, counts, width_out, offset, bands_out)
        current = jnp.where(live_rows[:, None], lower_values + delayed, jnp.zeros_like(delayed))
    return current


MESH = pl.DeviceIdType.MESH


def kernel(
    tiles, tm_size, x_ref, lower, upper, delays, counts, select, order,
    out_ref, raw, mine, cur, own_in, far_in, far_pass, halo_in, halo_pass,
    picked, land, early, joined, final,
    s_raw, s_far, s_far_pass, s_own, s_halo, s_halo_pass, s_fo, s_no, s_fi, s_edge,
):
    f, t = lax.axis_index("freq"), lax.axis_index("tm")
    c, z = lax.rem(f, 2), lax.div(f, 2)
    zb, half = lax.rem(z, 2), lax.div(z, 2)
    rows = x_ref.shape[0]
    chunk = CHUNK_ROWS
    n = rows // chunk
    at = lambda ff, tt: {"freq": ff, "tm": tt}
    partner = at(f + 1 - 2 * c, t)
    near = at(f + 2 - 4 * zb, t)
    across = at(f + 4 - 8 * half, t)
    facing = at(f + 2 - 4 * half, t)
    later = at(f, t + 1)
    earlier = at(f, t - 1)
    inner = zb != half
    outer = zb == half
    has_later, has_earlier = t < tm_size - 1, t > 0

    barrier = pltpu.get_barrier_semaphore()

    def greet(target):
        pl.semaphore_signal(barrier, inc=1, device_id=target, device_id_type=MESH)

    greet(partner)
    greet(near)
    greet(across)
    for cond, target in ((inner, facing), (has_earlier, earlier), (has_later, later)):
        pl.when(cond)(functools.partial(greet, target))
    one = lambda cond: jnp.where(cond, 1, 0)
    pl.semaphore_wait(barrier, 3 + one(inner) + one(has_earlier) + one(has_later))

    lane = lax.broadcasted_iota(jnp.int32, (tiles, LANES), 1)
    zero = jnp.zeros((tiles, LANES), jnp.float32)

    def when(cond, action):
        pl.when(cond)(action)

    def remote(src, dst, sems, j, target):
        return pltpu.make_async_remote_copy(
            src_ref=src, dst_ref=dst, send_sem=sems.at[0, j], recv_sem=sems.at[1, j],
            device_id=target, device_id_type=MESH,
        )

    def span(j):
        return pl.ds(pl.multiple_of(j * chunk, chunk), chunk)

    def delayed(source, row, d, first):
        q, r = d >> 7, d & (LANES - 1)
        a = source[row, pl.ds(tiles - q, tiles), :]
        b = source[row, pl.ds(jnp.maximum(tiles - 1 - q, first), tiles), :]
        a, b = pltpu.roll(a, r, 1), pltpu.roll(b, r, 1)
        return jnp.where(lane >= r, a, b)

    def blocks(start, count, value, store):
        def body(step, carry):
            base = start + step * UNROLL
            values = [(base + u, value(base + u)) for u in range(UNROLL)]
            for m, v in values:
                store(m, v)
            return carry

        if count == UNROLL:
            body(0, 0)
        else:
            lax.fori_loop(0, count // UNROLL, body, 0)

    rim0 = rows // LANES
    n0, chunk0 = CHUNKS_0, rows // CHUNKS_0

    def raw_copy(kind, j, row, target, source_at, target_at, size):
        span0 = pl.ds(row + j * chunk0, chunk0)
        return remote(
            raw.at[span0, pl.ds(source_at, size)], raw.at[span0, pl.ds(target_at, size)],
            s_raw, kind * n0 + j, target,
        )

    tail0 = (2 * tiles - rim0, tiles - rim0, rim0)
    kept0 = (tiles - rim0, tiles - rim0, rim0)
    full0 = (tiles, tiles, tiles)
    own0 = lambda j, row: raw_copy(0, j, row, partner, *full0)
    rim_out0 = lambda j: raw_copy(1, j, rows, later, *tail0)
    rim_in0 = lambda j: raw_copy(2, j, rows, partner, *kept0)

    def spread(first, count):
        def body(step, carry):
            r = first + step * SUBLANES
            for tile in range(tiles):
                raw[pl.ds(c * rows + r, SUBLANES), tiles + tile, :] = x_ref[
                    pl.ds(r, SUBLANES), pl.ds(tile * LANES, LANES)
                ]
            return carry

        lax.fori_loop(0, count // SUBLANES, body, 0)

    for j in range(n0):
        spread(j * chunk0, chunk0)
        when((c == 1) & has_later, rim_out0(j).start)
        own0(j, c * rows).start()

    def clear(count, store):
        def body(i, carry):
            for u in range(UNROLL):
                store(i * UNROLL + u)
            return carry

        lax.fori_loop(0, count // UNROLL, body, 0)

    @pl.when(t == 0)
    def _():
        def clear_raw(i):
            raw[rows + i, :tiles, :] = zero

        def clear_cur(i):
            cur[2 * rows + i, :tiles, :] = zero

        def clear_early(i):
            early[i] = zero

        clear(rows, clear_raw)
        clear(2 * rows, clear_cur)
        clear(rows, clear_early)

    for j in range(n0):

        @pl.when((c == 1) & has_earlier)
        def _():
            rim_out0(j).wait_recv()
            rim_in0(j).start()

    for j in range(n0):
        own0(j, (1 - c) * rows).wait_recv()
        when((c == 0) & has_earlier, rim_in0(j).wait_recv)

    own_base, far_base = zb * 2 * rows, (1 - zb) * 2 * rows
    up_base = 2 * rows
    limit0 = counts[z]

    def value0(m):
        i = order[zb, c * rows + m]
        g = z * 2 * rows + i
        wrap = 2 * rows - 1
        lo, up, d = lower[0, g] & wrap, upper[0, g] & wrap, delays[0, g]
        total = raw[lo, tiles:, :] + delayed(raw, up, d, tiles - rim0)
        return jnp.where(i < limit0, total, zero)

    def store0(m, v):
        mine[m] = v
        cur[own_base + c * rows + m, tiles:, :] = v

    limit1 = counts[2 ** (ITERS - 1) + half]
    rim1 = 2 * rows // LANES

    def value1(target_f):
        def value(m):
            j = select[target_f * rows + m]
            wrap = 2 * rows - 1
            a, b = order[2, lower[1, j] & wrap], order[3, upper[1, j] & wrap]
            total = cur[a, tiles:, :] + delayed(cur, up_base + b, delays[1, j], tiles - rim1)
            return jnp.where((j & (4 * rows - 1)) < limit1, total, zero)

        return value

    def store_picked(kind):
        def store(m, v):
            picked[kind, m] = v

        return store

    def store_land(m, v):
        land[half, m] = v

    limit2 = counts[2**ITERS - 2]

    def join(m):
        joined[m, :tiles, :] = early[m]
        joined[m, tiles:, :] = land[1, m]

    def value2(m):
        g = f * rows + m
        total = land[0, m] + delayed(joined, m, delays[2, g], 0)
        return jnp.where(g < limit2, total, zero)

    def store2(m, v):
        final[m] = v

    def finish(k):
        start = pl.multiple_of(k * chunk, chunk)
        for u in range(chunk):
            join(start + u)
        blocks(start, chunk, value2, store2)
        for step in range(chunk // SUBLANES):
            r = pl.multiple_of(start + step * SUBLANES, SUBLANES)
            for tile in range(tiles):
                out_ref[pl.ds(r, SUBLANES), pl.ds(tile * LANES, LANES)] = final[pl.ds(r, SUBLANES), tile, :]

    rim = pl.ds(tiles - rim1, rim1)
    far = lambda j: remote(mine.at[span(j)], far_in.at[span(j)], s_far, j, near)
    far_on = lambda j: remote(far_in.at[span(j)], far_pass.at[span(j)], s_far_pass, j, partner)
    own1 = lambda j: remote(mine.at[span(j)], own_in.at[span(j)], s_own, j, partner)
    halo_mine = lambda j: remote(mine.at[span(j), rim], halo_in.at[span(j), rim], s_halo, j, later)
    halo_far = lambda j: remote(far_in.at[span(j), rim], halo_in.at[span(j), rim], s_halo, j, later)
    halo_on = lambda j: remote(halo_in.at[span(j), rim], halo_pass.at[span(j), rim], s_halo_pass, j, partner)
    far_outer = lambda j, h: remote(picked.at[0, span(j)], land.at[h, span(j)], s_fo, j, across)
    near_outer = lambda j, h: remote(picked.at[1, span(j)], land.at[h, span(j)], s_no, j, near)
    far_inner = lambda j, h: remote(picked.at[2, span(j)], land.at[h, span(j)], s_fi, j, facing)
    edge = lambda j: remote(land.at[1, span(j)], early.at[span(j)], s_edge, j, later)

    def loop(count, body):
        def step(j, carry):
            body(j)
            return carry

        lax.fori_loop(0, count, step, 0)

    f_across, f_near, f_facing = f + 4 - 8 * half, f + 2 - 4 * zb, f + 2 - 4 * half

    def finish_lagged(j):
        @pl.when(j >= EDGE_LAG)
        def _():
            k = j - EDGE_LAG
            when(has_earlier, edge(k).wait_recv)
            finish(k)

    @pl.when(outer)
    def _():
        def produce(j):
            blocks(j * chunk, chunk, value0, store0)
            far(j).start()

        loop(n, produce)

        def from_across(j):
            far_outer(j, 1 - half).wait_recv()
            when((half == 0) & has_later, edge(j).start)

        loop(n, from_across)

        def from_near(j):
            @pl.when(j < n)
            def _():
                near_outer(j, half).wait_recv()
                when((half == 1) & has_later, edge(j).start)

            finish_lagged(j)

        loop(n + EDGE_LAG, from_near)

        def drain(j):
            far(j).wait_send()
            when(has_later, edge(j).wait_send)

        loop(n, drain)

    @pl.when(inner)
    def _():
        def produce(j):
            blocks(j * chunk, chunk, value0, store0)
            own1(j).start()
            when((half == 0) & has_later, halo_mine(j).start)

        loop(n, produce)

        def gather(k):
            far_on(k).wait_recv()
            own1(k).wait_recv()
            start = pl.multiple_of(k * chunk, chunk)
            mine_at, other_at = c * rows + start, (1 - c) * rows + start
            for u in range(chunk):
                cur[own_base + other_at + u, tiles:, :] = own_in[start + u]
                cur[far_base + mine_at + u, tiles:, :] = far_in[start + u]
                cur[far_base + other_at + u, tiles:, :] = far_pass[start + u]

            @pl.when(has_earlier)
            def _():
                halo_on(k).wait_recv()
                for u in range(chunk):
                    cur[up_base + mine_at + u, :tiles, :] = halo_in[start + u]
                    cur[up_base + other_at + u, :tiles, :] = halo_pass[start + u]

            blocks(k * chunk, chunk, value1(f_across), store_picked(0))
            far_outer(k, half).start()

        def stream(j):
            @pl.when(j < n)
            def _():
                far(j).wait_recv()
                far_on(j).start()
                when((half == 1) & has_later, halo_far(j).start)

            @pl.when((j >= HALO_LAG) & (j < n + HALO_LAG) & has_earlier)
            def _():
                halo_mine(j - HALO_LAG).wait_recv()
                halo_on(j - HALO_LAG).start()

            @pl.when(j >= MERGE_LAG)
            def _():
                gather(j - MERGE_LAG)

        loop(n + MERGE_LAG, stream)

        def rest(j):
            blocks(j * chunk, chunk, value1(f_facing), store_picked(2))
            far_inner(j, half).start()
            blocks(j * chunk, chunk, value1(f_near), store_picked(1))
            near_outer(j, half).start()
            blocks(j * chunk, chunk, value1(f), store_land)
            when((half == 1) & has_later, edge(j).start)

        loop(n, rest)

        def receive(j):
            @pl.when(j < n)
            def _():
                far_inner(j, 1 - half).wait_recv()
                when((half == 0) & has_later, edge(j).start)

            finish_lagged(j)

        loop(n + EDGE_LAG, receive)

        def drain(j):
            own1(j).wait_send()
            far_on(j).wait_send()
            when(has_later, halo_mine(j).wait_send)
            when(has_earlier, halo_on(j).wait_send)
            far_outer(j, half).wait_send()
            near_outer(j, half).wait_send()
            far_inner(j, half).wait_send()
            when(has_later, edge(j).wait_send)

        loop(n, drain)

    for j in range(n0):
        own0(j, c * rows).wait_send()
        when((c == 1) & has_later, rim_out0(j).wait_send)
        when((c == 1) & has_earlier, rim_in0(j).wait_send)


def first_use_order(lower_rows, upper_rows, row_count):
    half = lax.axis_index("freq") // 4
    chip_rows, half_rows = 2 * row_count, 4 * row_count
    select = jnp.where(half == 0, lower_rows[2], upper_rows[2])
    wanted = jnp.where(half == 0, select[3 * chip_rows :], select[:chip_rows])
    wanted = wanted.reshape(2, row_count).T.reshape(-1) & (half_rows - 1)
    tables = jnp.stack([lower_rows[1], upper_rows[1]]).reshape(2, 2, half_rows)
    tables = jnp.where(half == 0, tables[:, 0], tables[:, 1]) & (chip_rows - 1)
    at_half = jnp.arange(half_rows, dtype=jnp.int32)
    at_chip = jnp.arange(chip_rows, dtype=jnp.int32)
    hit = wanted[:, None] == at_half[None, :]
    used = jnp.sum(jnp.where(hit[None], tables[:, None, :], 0), axis=2)
    same = used[:, :, None] == at_chip[None, None, :]
    first = jnp.min(jnp.where(same, at_chip[None, :, None], chip_rows), axis=1)
    key = first * chip_rows + at_chip[None, :]
    rank = jnp.sum((key[:, None, :] < key[:, :, None]).astype(jnp.int32), axis=2)
    place = (rank % 2) * row_count + rank // 2
    holds = place[:, :, None] == at_chip[None, None, :]
    row_at = jnp.sum(jnp.where(holds, at_chip[None, :, None], 0), axis=1)
    return select, jnp.concatenate([row_at, place], axis=0)


def per_device_fused(tm_size, band_state, lower_rows, upper_rows, delays, counts):
    row_count, samples = band_state.shape
    tiles = samples // LANES
    n = row_count // CHUNK_ROWS
    dma = pltpu.SemaphoreType.DMA
    wide = pltpu.VMEM((row_count, tiles, LANES), jnp.float32)
    select, order = first_use_order(lower_rows, upper_rows, row_count)
    return pl.pallas_call(
        functools.partial(kernel, tiles, tm_size),
        out_shape=jax.ShapeDtypeStruct((row_count, samples), jnp.float32),
        in_specs=[pl.BlockSpec(memory_space=pltpu.VMEM)] + [pl.BlockSpec(memory_space=pltpu.SMEM)] * 6,
        out_specs=pl.BlockSpec(memory_space=pltpu.VMEM),
        scratch_shapes=[
            pltpu.VMEM((2 * row_count, 2 * tiles, LANES), jnp.float32),
            wide,
            pltpu.VMEM((4 * row_count, 2 * tiles, LANES), jnp.float32),
            wide, wide, wide, wide, wide,
            pltpu.VMEM((3, row_count, tiles, LANES), jnp.float32),
            pltpu.VMEM((2, row_count, tiles, LANES), jnp.float32),
            wide,
            pltpu.VMEM((row_count, 2 * tiles, LANES), jnp.float32),
            wide,
            dma((2, 3 * CHUNKS_0)),
        ]
        + [dma((2, n))] * 9,
        compiler_params=pltpu.CompilerParams(
            collective_id=0, has_side_effects=True, vmem_limit_bytes=60 * 2**20
        ),
    )(band_state, lower_rows, upper_rows, delays, counts, select, order)


def solution(mesh):
    if mesh.shape["freq"] == 2**ITERS:
        body = functools.partial(per_device_fused, mesh.shape["tm"])
    else:
        body = per_device_general
    return jax.shard_map(
        body,
        mesh=mesh,
        in_specs=(P("freq", "tm"), P(), P(), P(), P()),
        out_specs=P("freq", "tm"),
        check_vma=False,
    )
```

time: 106 us -> 81.5 us (0.77)
  the two profiles are of different devices: /device:TPU:7 before, /device:TPU:12 now
where the time goes in v1:
time: 81.5 us; the launch traced here: 81.2 us
  Pallas kernels  74.8 us (92%)
  other arithmetic  3.66 us (4%)
  local copies, waits for them, and re-layouts  2.64 us (3%)
    pallas_call x1, Pallas kernels, per_device_fused(): pl.pallas_call(functools.partial(kernel, tiles, tm_size), out_shape=jax.S...  74.8 us
    unnamed x4, local copies, waits for them, and re-layouts  2.32 us

profile of v1, /device:TPU:12, one launch (start us, length us, event | category | flops | bytes accessed | tf_op | source)
XLA Modules:
  0.0 81.2 jit_solution(17629139273236737256)
XLA Ops:
  0.0 0.9 %fusion.5 = (s32[1,2048]{1,0:T(1,128)S(1)}, s32[1,2048]{1,0:T(1,128)S(1)}, s32[1,2048]{1,0:T(1,128)S(1)}) fusion(s32[3,2048]{1,0:T(4,128)} %lower.1, s32[3,2048]{1,0:T(4,128)} %upper.1, pred[]{:T(512)S(6)} %eq.50), kind=kLoop, calls=%fused_computation.24 | loop fusion | flops 2048 | bytes 57345 | tf_op jit(solution)/shard_map/slice | solution.py:424
  0.9 0.0 copy-start
  1.0 0.1 copy.7
  1.2 0.1 and.63
  1.3 0.4 iota_compare_fusion.2
  1.7 0.7 select_reduce_fusion
  2.4 0.4 select_reduce_fusion.2
  2.7 0.4 convert_reduce_fusion
  3.2 0.3 select_reduce_fusion.1
  3.5 0.6 pad_add_fusion.1.order
  4.1 0.0 copy-done
  4.1 74.8 %shard_map.55 = f32[256,1024]{1,0:T(8,128)} custom-call(f32[256,1024]{1,0:T(8,128)} %x_ref.1, s32[3,2048]{1,0:T(4,128)} %lower.1, s32[3,2048]{1,0:T(4,128)} %upper.1, s32[3,2048]{1,0:T(4,128)} %delays.1, s32[7]{0:T(128)} %counts.1, s32[2048]{0:T(1024)} %bitcast.6, s32[4,512]{1,0:T(4,128)} %pad_add_fusion.1.order), custom_call_target="tpu_custom_call" | custom-call | tf_op jit(solution)/shard_map/pallas_call | solution.py:447
  78.9 2.3 %copy.12 = f32[256,1024]{1,0:T(8,128)} copy(f32[256,1024]{1,0:T(8,128)} %shard_map.55) | data formatting | bytes 2097152
  (8 shorter events, 0.1 us)
Async XLA Ops:
  0.9 3.2 %copy-start = (s32[1,2048]{1,0:T(1,128)}, s32[1,2048]{1,0:T(1,128)S(1)}, u32[]{:S(2)}) copy-start(s32[1,2048]{1,0:T(1,128)S(1)} %get-tuple-element.6) | copy-start | bytes 24580

commit v2 on v1

--- a/solution.py
+++ b/solution.py
@@ -1,3 +1,4 @@
+import contextlib
 import functools
 
 import jax
@@ -16,7 +17,10 @@
 CHUNK_ROWS = 16
 HALO_LAG = 2
 MERGE_LAG = 3
-EDGE_LAG = 2
+OWN_GROUP = 4
+OUTER_GROUP = 4
+NEAR_GROUP = 2
+EDGE_LAG = 4
 
 
 def shifted_2(block, axis, distance):
@@ -72,11 +76,15 @@
 MESH = pl.DeviceIdType.MESH
 
 
+def phase(name):
+    return contextlib.nullcontext()
+
+
 def kernel(
     tiles, tm_size, x_ref, lower, upper, delays, counts, select, order,
     out_ref, raw, mine, cur, own_in, far_in, far_pass, halo_in, halo_pass,
     picked, land, early, joined, final,
-    s_raw, s_far, s_far_pass, s_own, s_halo, s_halo_pass, s_fo, s_no, s_fi, s_edge,
+    sent, s_raw, s_far, s_far_pass, s_own, s_halo, s_halo_pass, s_fo, s_no, s_fi, s_edge,
 ):
     f, t = lax.axis_index("freq"), lax.axis_index("tm")
     c, z = lax.rem(f, 2), lax.div(f, 2)
@@ -105,8 +113,6 @@
     greet(across)
     for cond, target in ((inner, facing), (has_earlier, earlier), (has_later, later)):
         pl.when(cond)(functools.partial(greet, target))
-    one = lambda cond: jnp.where(cond, 1, 0)
-    pl.semaphore_wait(barrier, 3 + one(inner) + one(has_earlier) + one(has_later))
 
     lane = lax.broadcasted_iota(jnp.int32, (tiles, LANES), 1)
     zero = jnp.zeros((tiles, LANES), jnp.float32)
@@ -114,14 +120,14 @@
     def when(cond, action):
         pl.when(cond)(action)
 
-    def remote(src, dst, sems, j, target):
+    def remote(src, dst, flow, sem, target):
         return pltpu.make_async_remote_copy(
-            src_ref=src, dst_ref=dst, send_sem=sems.at[0, j], recv_sem=sems.at[1, j],
+            src_ref=src, dst_ref=dst, send_sem=sent.at[flow], recv_sem=sem,
             device_id=target, device_id_type=MESH,
         )
 
-    def span(j):
-        return pl.ds(pl.multiple_of(j * chunk, chunk), chunk)
+    def span(j, group=1):
+        return pl.ds(pl.multiple_of(j * chunk * group, chunk * group), chunk * group)
 
     def delayed(source, row, d, first):
         q, r = d >> 7, d & (LANES - 1)
@@ -150,7 +156,7 @@
         span0 = pl.ds(row + j * chunk0, chunk0)
         return remote(
             raw.at[span0, pl.ds(source_at, size)], raw.at[span0, pl.ds(target_at, size)],
-            s_raw, kind * n0 + j, target,
+            kind, s_raw.at[kind * n0 + j], target,
         )
 
     tail0 = (2 * tiles - rim0, tiles - rim0, rim0)
@@ -171,10 +177,15 @@
 
         lax.fori_loop(0, count // SUBLANES, body, 0)
 
-    for j in range(n0):
-        spread(j * chunk0, chunk0)
-        when((c == 1) & has_later, rim_out0(j).start)
-        own0(j, c * rows).start()
+    with phase("spread"):
+        spread(0, rows)
+    one = lambda cond: jnp.where(cond, 1, 0)
+    with phase("greet"):
+        pl.semaphore_wait(barrier, 3 + one(inner) + one(has_earlier) + one(has_later))
+    with phase("send0"):
+        for j in range(n0):
+            when((c == 1) & has_later, rim_out0(j).start)
+            own0(j, c * rows).start()
 
     def clear(count, store):
         def body(i, carry):
@@ -203,12 +214,15 @@
 
         @pl.when((c == 1) & has_earlier)
         def _():
-            rim_out0(j).wait_recv()
-            rim_in0(j).start()
+            with phase("rim_out"):
+                rim_out0(j).wait_recv()
+                rim_in0(j).start()
 
     for j in range(n0):
-        own0(j, (1 - c) * rows).wait_recv()
-        when((c == 0) & has_earlier, rim_in0(j).wait_recv)
+        with phase("own0"):
+            own0(j, (1 - c) * rows).wait_recv()
+        with phase("rim_in"):
+            when((c == 0) & has_earlier, rim_in0(j).wait_recv)
 
     own_base, far_base = zb * 2 * rows, (1 - zb) * 2 * rows
     up_base = 2 * rows
@@ -273,20 +287,33 @@
                 out_ref[pl.ds(r, SUBLANES), pl.ds(tile * LANES, LANES)] = final[pl.ds(r, SUBLANES), tile, :]
 
     rim = pl.ds(tiles - rim1, rim1)
-    far = lambda j: remote(mine.at[span(j)], far_in.at[span(j)], s_far, j, near)
-    far_on = lambda j: remote(far_in.at[span(j)], far_pass.at[span(j)], s_far_pass, j, partner)
-    own1 = lambda j: remote(mine.at[span(j)], own_in.at[span(j)], s_own, j, partner)
-    halo_mine = lambda j: remote(mine.at[span(j), rim], halo_in.at[span(j), rim], s_halo, j, later)
-    halo_far = lambda j: remote(far_in.at[span(j), rim], halo_in.at[span(j), rim], s_halo, j, later)
-    halo_on = lambda j: remote(halo_in.at[span(j), rim], halo_pass.at[span(j), rim], s_halo_pass, j, partner)
-    far_outer = lambda j, h: remote(picked.at[0, span(j)], land.at[h, span(j)], s_fo, j, across)
-    near_outer = lambda j, h: remote(picked.at[1, span(j)], land.at[h, span(j)], s_no, j, near)
-    far_inner = lambda j, h: remote(picked.at[2, span(j)], land.at[h, span(j)], s_fi, j, facing)
-    edge = lambda j: remote(land.at[1, span(j)], early.at[span(j)], s_edge, j, later)
-
-    def loop(count, body):
+    every = pl.ds(0, rows)
+
+    def flow(index, src, dst, sems, target):
+        def copy(j, group=1, sem=None):
+            at_rows = span(j, group)
+            return remote(src(at_rows), dst(at_rows), index, sems.at[j if sem is None else sem], target)
+
+        return copy, remote(src(every), dst(every), index, sems.at[0], target)
+
+    far, far_all = flow(3, lambda r: mine.at[r], lambda r: far_in.at[r], s_far, near)
+    far_on, far_on_all = flow(4, lambda r: far_in.at[r], lambda r: far_pass.at[r], s_far_pass, partner)
+    own1, own1_all = flow(5, lambda r: mine.at[r], lambda r: own_in.at[r], s_own, partner)
+    halo_mine, halo_all = flow(6, lambda r: mine.at[r, rim], lambda r: halo_in.at[r, rim], s_halo, later)
+    halo_far, _ = flow(6, lambda r: far_in.at[r, rim], lambda r: halo_in.at[r, rim], s_halo, later)
+    halo_on, halo_on_all = flow(7, lambda r: halo_in.at[r, rim], lambda r: halo_pass.at[r, rim], s_halo_pass, partner)
+    to_half = lambda h: lambda r: land.at[h, r]
+    far_outer, far_outer_all = flow(8, lambda r: picked.at[0, r], to_half(half), s_fo, across)
+    near_outer, near_outer_all = flow(9, lambda r: picked.at[1, r], to_half(half), s_no, near)
+    far_inner, far_inner_all = flow(10, lambda r: picked.at[2, r], to_half(half), s_fi, facing)
+    got_across, _ = flow(8, lambda r: picked.at[0, r], to_half(1 - half), s_fo, across)
+    got_facing, _ = flow(10, lambda r: picked.at[2, r], to_half(1 - half), s_fi, facing)
+    edge, edge_all = flow(11, lambda r: land.at[1, r], lambda r: early.at[r], s_edge, later)
+
+    def loop(name, count, body):
         def step(j, carry):
-            body(j)
+            with phase(name):
+                body(j)
             return carry
 
         lax.fori_loop(0, count, step, 0)
@@ -306,42 +333,48 @@
             blocks(j * chunk, chunk, value0, store0)
             far(j).start()
 
-        loop(n, produce)
+        loop("produce", n, produce)
 
         def from_across(j):
-            far_outer(j, 1 - half).wait_recv()
-            when((half == 0) & has_later, edge(j).start)
-
-        loop(n, from_across)
+            got_across(j, OUTER_GROUP).wait_recv()
+            for i in range(OUTER_GROUP):
+                when((half == 0) & has_later, edge(j * OUTER_GROUP + i).start)
+
+        loop("from_across", n // OUTER_GROUP, from_across)
 
         def from_near(j):
             @pl.when(j < n)
             def _():
-                near_outer(j, half).wait_recv()
+                @pl.when(lax.rem(j, NEAR_GROUP) == 0)
+                def _():
+                    near_outer(lax.div(j, NEAR_GROUP), NEAR_GROUP).wait_recv()
+
                 when((half == 1) & has_later, edge(j).start)
 
             finish_lagged(j)
 
-        loop(n + EDGE_LAG, from_near)
-
-        def drain(j):
-            far(j).wait_send()
-            when(has_later, edge(j).wait_send)
-
-        loop(n, drain)
+        loop("from_near", n + EDGE_LAG, from_near)
+
+        with phase("drain"):
+            far_all.wait_send()
+            when(has_later, edge_all.wait_send)
 
     @pl.when(inner)
     def _():
         def produce(j):
-            blocks(j * chunk, chunk, value0, store0)
-            own1(j).start()
-            when((half == 0) & has_later, halo_mine(j).start)
-
-        loop(n, produce)
+            for i in range(OWN_GROUP):
+                blocks((j * OWN_GROUP + i) * chunk, chunk, value0, store0)
+                when((half == 0) & has_later, halo_mine(j * OWN_GROUP + i).start)
+            own1(j, OWN_GROUP).start()
+
+        loop("produce", n // OWN_GROUP, produce)
 
         def gather(k):
+            @pl.when(lax.rem(k, OWN_GROUP) == 0)
+            def _():
+                own1(lax.div(k, OWN_GROUP), OWN_GROUP).wait_recv()
+
             far_on(k).wait_recv()
-            own1(k).wait_recv()
             start = pl.multiple_of(k * chunk, chunk)
             mine_at, other_at = c * rows + start, (1 - c) * rows + start
             for u in range(chunk):
@@ -357,7 +390,7 @@
                     cur[up_base + other_at + u, :tiles, :] = halo_pass[start + u]
 
             blocks(k * chunk, chunk, value1(f_across), store_picked(0))
-            far_outer(k, half).start()
+            far_outer(k, 1, lax.div(k, OUTER_GROUP)).start()
 
         def stream(j):
             @pl.when(j < n)
@@ -375,44 +408,47 @@
             def _():
                 gather(j - MERGE_LAG)
 
-        loop(n + MERGE_LAG, stream)
+        loop("stream", n + MERGE_LAG, stream)
 
         def rest(j):
-            blocks(j * chunk, chunk, value1(f_facing), store_picked(2))
-            far_inner(j, half).start()
-            blocks(j * chunk, chunk, value1(f_near), store_picked(1))
-            near_outer(j, half).start()
-            blocks(j * chunk, chunk, value1(f), store_land)
-            when((half == 1) & has_later, edge(j).start)
-
-        loop(n, rest)
+            for i in range(NEAR_GROUP):
+                k = j * NEAR_GROUP + i
+                blocks(k * chunk, chunk, value1(f_facing), store_picked(2))
+                far_inner(k).start()
+                blocks(k * chunk, chunk, value1(f_near), store_picked(1))
+                blocks(k * chunk, chunk, value1(f), store_land)
+                when((half == 1) & has_later, edge(k).start)
+            near_outer(j, NEAR_GROUP).start()
+
+        loop("rest", n // NEAR_GROUP, rest)
 
         def receive(j):
             @pl.when(j < n)
             def _():
-                far_inner(j, 1 - half).wait_recv()
+                got_facing(j).wait_recv()
                 when((half == 0) & has_later, edge(j).start)
 
             finish_lagged(j)
 
-        loop(n + EDGE_LAG, receive)
-
-        def drain(j):
-            own1(j).wait_send()
-            far_on(j).wait_send()
-            when(has_later, halo_mine(j).wait_send)
-            when(has_earlier, halo_on(j).wait_send)
-            far_outer(j, half).wait_send()
-            near_outer(j, half).wait_send()
-            far_inner(j, half).wait_send()
-            when(has_later, edge(j).wait_send)
-
-        loop(n, drain)
-
-    for j in range(n0):
-        own0(j, c * rows).wait_send()
-        when((c == 1) & has_later, rim_out0(j).wait_send)
-        when((c == 1) & has_earlier, rim_in0(j).wait_send)
+        loop("receive", n + EDGE_LAG, receive)
+
+        with phase("drain"):
+            own1_all.wait_send()
+            far_on_all.wait_send()
+            when(has_later, halo_all.wait_send)
+            when(has_earlier, halo_on_all.wait_send)
+            far_outer_all.wait_send()
+            near_outer_all.wait_send()
+            far_inner_all.wait_send()
+            when(has_later, edge_all.wait_send)
+
+    raw_all = lambda kind, row, target, source_at, target_at, size: remote(
+        raw.at[pl.ds(row, rows), pl.ds(source_at, size)], raw.at[pl.ds(row, rows), pl.ds(target_at, size)],
+        kind, s_raw.at[0], target,
+    )
+    raw_all(0, c * rows, partner, *full0).wait_send()
+    when((c == 1) & has_later, raw_all(1, rows, later, *tail0).wait_send)
+    when((c == 1) & has_earlier, raw_all(2, rows, partner, *kept0).wait_send)
 
 
 def first_use_order(lower_rows, upper_rows, row_count):
@@ -459,11 +495,20 @@
             wide,
             pltpu.VMEM((row_count, 2 * tiles, LANES), jnp.float32),
             wide,
-            dma((2, 3 * CHUNKS_0)),
-        ]
-        + [dma((2, n))] * 9,
+            dma((12,)),
+            dma((3 * CHUNKS_0,)),
+            dma((n,)),
+            dma((n,)),
+            dma((n // OWN_GROUP,)),
+            dma((n,)),
+            dma((n,)),
+            dma((n // OUTER_GROUP,)),
+            dma((n // NEAR_GROUP,)),
+            dma((n,)),
+            dma((n,)),
+        ],
         compiler_params=pltpu.CompilerParams(
-            collective_id=0, has_side_effects=True, vmem_limit_bytes=60 * 2**20
+            collective_id=0, has_side_effects=True, vmem_limit_bytes=36 * 2**20
         ),
     )(band_state, lower_rows, upper_rows, delays, counts, select, order)
 

time: 81.5 us -> 76.3 us (0.936)
  Pallas kernels: 74.8 us -> 71.6 us
  local copies, waits for them, and re-layouts: 2.64 us -> 1.32 us
    pallas_call x1, Pallas kernels: 74.8 us -> 71.6 us  [per_device_fused(): pl.pallas_call(functools.partial(kernel, tiles, tm_size), out_shape=jax.S...]
    unnamed x4 -> x12, local copies, waits for them, and re-layouts: 2.32 us -> 1 us
where the time goes in v2:
time: 76.3 us; the launch traced here: 76.2 us
  Pallas kernels  71.6 us (94%)
  other arithmetic  3.13 us (4%)
  local copies, waits for them, and re-layouts  1.32 us (2%)
    pallas_call x1, Pallas kernels, per_device_fused(): pl.pallas_call(functools.partial(kernel, tiles, tm_size), out_shape=jax.S...  71.6 us

profile of v2, /device:TPU:12, one launch (start us, length us, event | category | flops | bytes accessed | tf_op | source)
XLA Modules:
  0.0 76.2 jit_solution(2620592231560140705)
XLA Ops:
  0.0 0.0 copy-start.2
  0.0 0.0 copy-start.1
  0.0 0.0 copy-start.4
  0.0 0.0 copy-start.3
  0.0 0.0 copy-start
  0.0 0.9 %fusion.5 = (s32[1,2048]{1,0:T(1,128)S(1)}, s32[1,2048]{1,0:T(1,128)S(1)}, s32[1,2048]{1,0:T(1,128)S(1)}) fusion(s32[3,2048]{1,0:T(4,128)} %lower.1, s32[3,2048]{1,0:T(4,128)} %upper.1, pred[]{:T(512)S(6)} %eq.50), kind=kLoop, calls=%fused_computation.24 | loop fusion | flops 2048 | bytes 57345 | tf_op jit(solution)/shard_map/slice | solution.py:460
  1.1 0.1 copy.7
  1.3 0.1 and.63
  1.4 0.4 iota_compare_fusion.2
  1.8 0.7 select_reduce_fusion
  2.5 0.4 select_reduce_fusion.2
  2.8 0.4 convert_reduce_fusion
  3.3 0.3 select_reduce_fusion.1
  3.6 0.0 copy-done.2
  3.6 0.0 copy-done.1
  3.6 0.0 copy-done.4
  3.6 0.0 copy-done.3
  3.6 0.0 copy-done
  3.6 71.6 %shard_map.55 = f32[256,1024]{1,0:T(8,128)S(1)} custom-call(f32[256,1024]{1,0:T(8,128)S(1)} %copy-done, s32[3,2048]{1,0:T(4,128)S(1)} %copy-done.1, s32[3,2048]{1,0:T(4,128)S(1)} %copy-done.2, s32[3,2048]{1,0:T(4,128)S(1)} %copy-done.3, s32[7]{0:T(128)S(1)} %copy-done.4, s32[2048]{0:T(1024)S(1)} %bitcast.5, s32[4,512]{1,0:T(4,128)S(1)} %pad_add_fusion.1.order), custom_call_target="tpu_custom_call" | custom-call | tf_op jit(solution)/shard_map/pallas_call | solution.py:483
  75.2 1.0 %copy.12 = f32[256,1024]{1,0:T(8,128)} copy(f32[256,1024]{1,0:T(8,128)S(1)} %shard_map.55) | data formatting | bytes 2097152
  (9 shorter events, 0.1 us)
Async XLA Ops:
  0.0 3.6 %copy-start.2 = (s32[3,2048]{1,0:T(4,128)S(1)}, s32[3,2048]{1,0:T(4,128)}, u32[]{:S(2)}) copy-start(s32[3,2048]{1,0:T(4,128)} %upper.1) | copy-start | bytes 73732
  0.0 3.6 %copy-start.1 = (s32[3,2048]{1,0:T(4,128)S(1)}, s32[3,2048]{1,0:T(4,128)}, u32[]{:S(2)}) copy-start(s32[3,2048]{1,0:T(4,128)} %lower.1) | copy-start | bytes 73732
  0.0 3.6 %copy-start.4 = (s32[7]{0:T(128)S(1)}, s32[7]{0:T(128)}, u32[]{:S(2)}) copy-start(s32[7]{0:T(128)} %counts.1) | copy-start | bytes 88
  0.0 3.6 %copy-start.3 = (s32[3,2048]{1,0:T(4,128)S(1)}, s32[3,2048]{1,0:T(4,128)}, u32[]{:S(2)}) copy-start(s32[3,2048]{1,0:T(4,128)} %delays.1) | copy-start | bytes 73732
  0.0 3.6 %copy-start = (f32[256,1024]{1,0:T(8,128)S(1)}, f32[256,1024]{1,0:T(8,128)}, u32[]{:S(2)}) copy-start(f32[256,1024]{1,0:T(8,128)} %x_ref.1) | copy-start | bytes 3145732

commit v3 on v2

--- a/solution.py
+++ b/solution.py
@@ -20,6 +20,7 @@
 OWN_GROUP = 4
 OUTER_GROUP = 4
 NEAR_GROUP = 2
+PLAN_UNROLL = 8
 EDGE_LAG = 4
 
 
@@ -81,10 +82,10 @@
 
 
 def kernel(
-    tiles, tm_size, x_ref, lower, upper, delays, counts, select, order,
-    out_ref, raw, mine, cur, own_in, far_in, far_pass, halo_in, halo_pass,
+    tiles, tm_size, x_ref, lower, upper, delays, counts,
+    out_ref, columns, columns_0, places, plan_v, plan, picks_v, picks, raw, mine, cur, own_in, far_in, far_pass, halo_in, halo_pass,
     picked, land, early, joined, final,
-    sent, s_raw, s_far, s_far_pass, s_own, s_halo, s_halo_pass, s_fo, s_no, s_fi, s_edge,
+    sent, s_plan, s_raw, s_far, s_far_pass, s_own, s_halo, s_halo_pass, s_fo, s_no, s_fi, s_edge,
 ):
     f, t = lax.axis_index("freq"), lax.axis_index("tm")
     c, z = lax.rem(f, 2), lax.div(f, 2)
@@ -139,7 +140,7 @@
     def blocks(start, count, value, store):
         def body(step, carry):
             base = start + step * UNROLL
-            values = [(base + u, value(base + u)) for u in range(UNROLL)]
+            values = [(base + u, value(base, u)) for u in range(UNROLL)]
             for m, v in values:
                 store(m, v)
             return carry
@@ -210,6 +211,137 @@
         clear(2 * rows, clear_cur)
         clear(rows, clear_early)
 
+    chip_rows, half_rows = 2 * rows, 4 * rows
+    flat = (SUBLANES, LANES)
+    lane_at = lax.broadcasted_iota(jnp.int32, flat, 1)
+    line_at = lax.broadcasted_iota(jnp.int32, flat, 0)
+    none = jnp.zeros(flat, jnp.int32)
+    groups = lambda count: range(count // LANES)
+
+    def row_of(table, level, start):
+        return jnp.broadcast_to(table[level : level + 1, pl.ds(pl.multiple_of(start, LANES), LANES)], flat)
+
+    def wanted(start):
+        return jnp.where(half == 0, row_of(lower, ITERS - 1, start), row_of(upper, ITERS - 1, start)) & (half_rows - 1)
+
+    def set_columns(target, start, row):
+        target[pl.ds(start, LANES), :] = jnp.broadcast_to(row[0:1], (LANES, LANES)).T
+
+    def fold(values, combine):
+        for s in (4, 2, 1):
+            values = [combine(v, pltpu.roll(v, s, 0)) for v in values]
+        return values
+
+    def scan(count, init, step):
+        def body(i, carry):
+            for u in range(PLAN_UNROLL):
+                at_row = (i * PLAN_UNROLL + u) * SUBLANES
+                carry = step(pl.multiple_of(at_row, SUBLANES), line_at + at_row, carry)
+            return carry
+
+        return lax.fori_loop(0, count // SUBLANES // PLAN_UNROLL, body, init)
+
+    add, least = lambda a, b: a + b, jnp.minimum
+    bit = lambda cond, place: jnp.where(cond, 1 << place, 0)
+
+    def find_order():
+        for g in groups(half_rows):
+            start = half * half_rows + g * LANES
+            low, high = row_of(lower, 1, start), row_of(upper, 1, start)
+            set_columns(columns, g * LANES, (low & (chip_rows - 1)) | (high & (chip_rows - 1)) << 9)
+        want = [wanted((1 - half) * 3 * chip_rows + g * LANES) for g in groups(chip_rows)]
+
+        def use(at_row, index, carry):
+            line = columns[pl.ds(at_row, SUBLANES), :]
+            return tuple(v + jnp.where(w == index, line, 0) for v, w in zip(carry, want))
+
+        used = fold(scan(half_rows, (none,) * len(want), use), add)
+        for g, row in enumerate(used):
+            set_columns(columns, g * LANES, row)
+
+        def meet(at_row, index, carry):
+            line = columns[pl.ds(at_row, SUBLANES), :]
+            low, high = line & (chip_rows - 1), line >> 9
+            turn = 2 * (index & (rows - 1)) + lax.div(index, rows)
+            hits = [(part, g) for part in (low, high) for g in groups(chip_rows)]
+            return tuple(
+                least(v, jnp.where(part == lane_at + g * LANES, turn, chip_rows)) for v, (part, g) in zip(carry, hits)
+            )
+
+        never = jnp.full(flat, chip_rows, jnp.int32)
+        first = fold(scan(chip_rows, (never,) * (2 * len(want)), meet), least)
+        keys = [v * chip_rows + lane_at + (g % len(want)) * LANES for g, v in enumerate(first)]
+        for g, row in enumerate(keys):
+            set_columns(columns, g * LANES, row)
+
+        def count(at_row, index, carry):
+            low = columns[pl.ds(at_row, SUBLANES), :]
+            high = columns[pl.ds(chip_rows + at_row, SUBLANES), :]
+            parts = [low] * len(want) + [high] * len(want)
+            return tuple(v + jnp.where(part < key, 1, 0) for v, part, key in zip(carry, parts, keys))
+
+        ranks = fold(scan(chip_rows, (none,) * len(keys), count), add)
+        place = [(v & 1) * rows + (v >> 1) for v in ranks]
+        for g in groups(chip_rows):
+            low, high = place[g], place[len(want) + g]
+            set_columns(places, g * LANES, low | high << 9)
+            start = z * chip_rows + g * LANES
+            low, high = row_of(lower, 0, start), row_of(upper, 0, start)
+            live = bit(lane_at + g * LANES < counts[z], 28)
+            word = (low & (chip_rows - 1)) | (high & (chip_rows - 1)) << 9 | row_of(delays, 0, start) << 18 | live
+            set_columns(columns_0, g * LANES, word)
+
+        def pick(at_row, index, carry):
+            line = places[pl.ds(at_row, SUBLANES), :]
+            own = jnp.where(zb == 0, line & (chip_rows - 1), line >> 9)
+            word = columns_0[pl.ds(at_row, SUBLANES), :]
+            return tuple(
+                v + jnp.where(own == lane_at + (c * rows + g * LANES), word, 0) for g, v in enumerate(carry)
+            )
+
+        words = fold(scan(chip_rows, (none,) * len(groups(rows)), pick), add)
+        for g, row in enumerate(words):
+            plan_v[pl.ds(g, 1), :] = row[0:1]
+            start = f * rows + g * LANES
+            live = bit(lane_at + start < counts[2**ITERS - 2], 12)
+            plan_v[pl.ds(rows // LANES + g, 1), :] = (row_of(delays, 2, start) | live)[0:1]
+        pltpu.make_async_copy(plan_v, plan, s_plan.at[0]).start()
+
+    def place_rows():
+        marks = [half * half_rows + g * LANES for g in groups(half_rows)]
+        low = [row_of(lower, 1, start) & (chip_rows - 1) for start in marks]
+        high = [row_of(upper, 1, start) & (chip_rows - 1) for start in marks]
+
+        def put(at_row, index, carry):
+            line = places[pl.ds(at_row, SUBLANES), :]
+            shifted = line >> 9 << 9
+            line = line & (chip_rows - 1)
+            return tuple(
+                v + jnp.where(a == index, line, 0) + jnp.where(b == index, shifted, 0)
+                for v, a, b in zip(carry, low, high)
+            )
+
+        words = fold(scan(chip_rows, (none,) * len(marks), put), add)
+        for g, (start, word) in enumerate(zip(marks, words)):
+            live = bit(lane_at + g * LANES < counts[2 ** (ITERS - 1) + half], 28)
+            set_columns(columns, g * LANES, word | row_of(delays, 1, start) << 18 | live)
+
+    def pick_rows():
+        targets = (f + 4 - 8 * half, f + 2 - 4 * zb, f + 2 - 4 * half, f)
+        want = [wanted(target * rows + g * LANES) for target in targets for g in groups(rows)]
+
+        def pick(at_row, index, carry):
+            line = columns[pl.ds(at_row, SUBLANES), :]
+            return tuple(v + jnp.where(w == index, line, 0) for v, w in zip(carry, want))
+
+        words = fold(scan(half_rows, (none,) * len(want), pick), add)
+        for g, row in enumerate(words):
+            picks_v[pl.ds(g, 1), :] = row[0:1]
+        pltpu.make_async_copy(picks_v, picks, s_plan.at[1]).start()
+
+    with phase("order"):
+        find_order()
+
     for j in range(n0):
 
         @pl.when((c == 1) & has_earlier)
@@ -224,32 +356,30 @@
         with phase("rim_in"):
             when((c == 0) & has_earlier, rim_in0(j).wait_recv)
 
+    pltpu.make_async_copy(plan_v, plan, s_plan.at[0]).wait()
     own_base, far_base = zb * 2 * rows, (1 - zb) * 2 * rows
     up_base = 2 * rows
-    limit0 = counts[z]
-
-    def value0(m):
-        i = order[zb, c * rows + m]
-        g = z * 2 * rows + i
-        wrap = 2 * rows - 1
-        lo, up, d = lower[0, g] & wrap, upper[0, g] & wrap, delays[0, g]
+    def entry(table, first, base, u):
+        return table[first + (base >> 7), (base & (LANES - 1)) + u]
+
+    def value0(base, u):
+        word = entry(plan, 0, base, u)
+        lo, up, d = word & 511, (word >> 9) & 511, (word >> 18) & 1023
         total = raw[lo, tiles:, :] + delayed(raw, up, d, tiles - rim0)
-        return jnp.where(i < limit0, total, zero)
+        return jnp.where((word >> 28) == 1, total, zero)
 
     def store0(m, v):
         mine[m] = v
         cur[own_base + c * rows + m, tiles:, :] = v
 
-    limit1 = counts[2 ** (ITERS - 1) + half]
     rim1 = 2 * rows // LANES
 
-    def value1(target_f):
-        def value(m):
-            j = select[target_f * rows + m]
-            wrap = 2 * rows - 1
-            a, b = order[2, lower[1, j] & wrap], order[3, upper[1, j] & wrap]
-            total = cur[a, tiles:, :] + delayed(cur, up_base + b, delays[1, j], tiles - rim1)
-            return jnp.where((j & (4 * rows - 1)) < limit1, total, zero)
+    def value1(kind):
+        def value(base, u):
+            word = entry(picks, kind * (rows // LANES), base, u)
+            a, b, d = word & 511, (word >> 9) & 511, (word >> 18) & 1023
+            total = cur[a, tiles:, :] + delayed(cur, up_base + b, d, tiles - rim1)
+            return jnp.where((word >> 28) == 1, total, zero)
 
         return value
 
@@ -262,16 +392,14 @@
     def store_land(m, v):
         land[half, m] = v
 
-    limit2 = counts[2**ITERS - 2]
-
     def join(m):
         joined[m, :tiles, :] = early[m]
         joined[m, tiles:, :] = land[1, m]
 
-    def value2(m):
-        g = f * rows + m
-        total = land[0, m] + delayed(joined, m, delays[2, g], 0)
-        return jnp.where(g < limit2, total, zero)
+    def value2(base, u):
+        word = entry(plan, rows // LANES, base, u)
+        total = land[0, base + u] + delayed(joined, base + u, word & 4095, 0)
+        return jnp.where((word >> 12) == 1, total, zero)
 
     def store2(m, v):
         final[m] = v
@@ -318,8 +446,6 @@
 
         lax.fori_loop(0, count, step, 0)
 
-    f_across, f_near, f_facing = f + 4 - 8 * half, f + 2 - 4 * zb, f + 2 - 4 * half
-
     def finish_lagged(j):
         @pl.when(j >= EDGE_LAG)
         def _():
@@ -389,7 +515,7 @@
                     cur[up_base + mine_at + u, :tiles, :] = halo_in[start + u]
                     cur[up_base + other_at + u, :tiles, :] = halo_pass[start + u]
 
-            blocks(k * chunk, chunk, value1(f_across), store_picked(0))
+            blocks(k * chunk, chunk, value1(0), store_picked(0))
             far_outer(k, 1, lax.div(k, OUTER_GROUP)).start()
 
         def stream(j):
@@ -399,11 +525,16 @@
                 far_on(j).start()
                 when((half == 1) & has_later, halo_far(j).start)
 
+            pl.when(j == 0)(place_rows)
+            pl.when(j == 1)(pick_rows)
+
             @pl.when((j >= HALO_LAG) & (j < n + HALO_LAG) & has_earlier)
             def _():
                 halo_mine(j - HALO_LAG).wait_recv()
                 halo_on(j - HALO_LAG).start()
 
+            when(j == MERGE_LAG, pltpu.make_async_copy(picks_v, picks, s_plan.at[1]).wait)
+
             @pl.when(j >= MERGE_LAG)
             def _():
                 gather(j - MERGE_LAG)
@@ -413,10 +544,10 @@
         def rest(j):
             for i in range(NEAR_GROUP):
                 k = j * NEAR_GROUP + i
-                blocks(k * chunk, chunk, value1(f_facing), store_picked(2))
+                blocks(k * chunk, chunk, value1(2), store_picked(2))
                 far_inner(k).start()
-                blocks(k * chunk, chunk, value1(f_near), store_picked(1))
-                blocks(k * chunk, chunk, value1(f), store_land)
+                blocks(k * chunk, chunk, value1(1), store_picked(1))
+                blocks(k * chunk, chunk, value1(3), store_land)
                 when((half == 1) & has_later, edge(k).start)
             near_outer(j, NEAR_GROUP).start()
 
@@ -451,41 +582,25 @@
     when((c == 1) & has_earlier, raw_all(2, rows, partner, *kept0).wait_send)
 
 
-def first_use_order(lower_rows, upper_rows, row_count):
-    half = lax.axis_index("freq") // 4
-    chip_rows, half_rows = 2 * row_count, 4 * row_count
-    select = jnp.where(half == 0, lower_rows[2], upper_rows[2])
-    wanted = jnp.where(half == 0, select[3 * chip_rows :], select[:chip_rows])
-    wanted = wanted.reshape(2, row_count).T.reshape(-1) & (half_rows - 1)
-    tables = jnp.stack([lower_rows[1], upper_rows[1]]).reshape(2, 2, half_rows)
-    tables = jnp.where(half == 0, tables[:, 0], tables[:, 1]) & (chip_rows - 1)
-    at_half = jnp.arange(half_rows, dtype=jnp.int32)
-    at_chip = jnp.arange(chip_rows, dtype=jnp.int32)
-    hit = wanted[:, None] == at_half[None, :]
-    used = jnp.sum(jnp.where(hit[None], tables[:, None, :], 0), axis=2)
-    same = used[:, :, None] == at_chip[None, None, :]
-    first = jnp.min(jnp.where(same, at_chip[None, :, None], chip_rows), axis=1)
-    key = first * chip_rows + at_chip[None, :]
-    rank = jnp.sum((key[:, None, :] < key[:, :, None]).astype(jnp.int32), axis=2)
-    place = (rank % 2) * row_count + rank // 2
-    holds = place[:, :, None] == at_chip[None, None, :]
-    row_at = jnp.sum(jnp.where(holds, at_chip[None, :, None], 0), axis=1)
-    return select, jnp.concatenate([row_at, place], axis=0)
-
-
 def per_device_fused(tm_size, band_state, lower_rows, upper_rows, delays, counts):
     row_count, samples = band_state.shape
     tiles = samples // LANES
     n = row_count // CHUNK_ROWS
     dma = pltpu.SemaphoreType.DMA
     wide = pltpu.VMEM((row_count, tiles, LANES), jnp.float32)
-    select, order = first_use_order(lower_rows, upper_rows, row_count)
     return pl.pallas_call(
         functools.partial(kernel, tiles, tm_size),
         out_shape=jax.ShapeDtypeStruct((row_count, samples), jnp.float32),
-        in_specs=[pl.BlockSpec(memory_space=pltpu.VMEM)] + [pl.BlockSpec(memory_space=pltpu.SMEM)] * 6,
+        in_specs=[pl.BlockSpec(memory_space=pltpu.VMEM)] * 4 + [pl.BlockSpec(memory_space=pltpu.SMEM)],
         out_specs=pl.BlockSpec(memory_space=pltpu.VMEM),
         scratch_shapes=[
+            pltpu.VMEM((4 * row_count, LANES), jnp.int32),
+            pltpu.VMEM((2 * row_count, LANES), jnp.int32),
+            pltpu.VMEM((2 * row_count, LANES), jnp.int32),
+            pltpu.VMEM((2 * row_count // LANES, LANES), jnp.int32),
+            pltpu.SMEM((2 * row_count // LANES, LANES), jnp.int32),
+            pltpu.VMEM((4 * row_count // LANES, LANES), jnp.int32),
+            pltpu.SMEM((4 * row_count // LANES, LANES), jnp.int32),
             pltpu.VMEM((2 * row_count, 2 * tiles, LANES), jnp.float32),
             wide,
             pltpu.VMEM((4 * row_count, 2 * tiles, LANES), jnp.float32),
@@ -496,6 +611,7 @@
             pltpu.VMEM((row_count, 2 * tiles, LANES), jnp.float32),
             wide,
             dma((12,)),
+            dma((2,)),
             dma((3 * CHUNKS_0,)),
             dma((n,)),
             dma((n,)),
@@ -510,7 +626,7 @@
         compiler_params=pltpu.CompilerParams(
             collective_id=0, has_side_effects=True, vmem_limit_bytes=36 * 2**20
         ),
-    )(band_state, lower_rows, upper_rows, delays, counts, select, order)
+    )(band_state, lower_rows, upper_rows, delays, counts)
 
 
 def solution(mesh):

time: 76.3 us -> 73.8 us (0.967)
  local copies, waits for them, and re-layouts: 1.32 us -> 5.12 us
  Pallas kernels: 71.6 us -> 68.2 us
  other arithmetic: 3.13 us -> 0 us
    unnamed x12 -> x11, local copies, waits for them, and re-layouts: 1 us -> 5.12 us
    pallas_call x1, Pallas kernels: 71.6 us -> 68.2 us  [per_device_fused(): pl.pallas_call(functools.partial(kernel, tiles, tm_size), out_shape=jax.S...]
    reduce_sum x3 -> x0, other arithmetic: 1.37 us -> none  [the longest x1 0.68 us: first_use_order(): used = jnp.sum(jnp.where(hit[None], tables[:, None, :], 0), axis=2)]
    slice x1 -> x0, other arithmetic: 0.93 us -> none  [first_use_order(): tables = jnp.stack([lower_rows[1], upper_rows[1]]).reshape(2, 2, half_rows)]
where the time goes in v3:
time: 73.8 us; the launch traced here: 73.3 us
  Pallas kernels  68.2 us (92%)
  local copies, waits for them, and re-layouts  5.12 us (7%)
    pallas_call x1, Pallas kernels, per_device_fused(): pl.pallas_call(functools.partial(kernel, tiles, tm_size), out_shape=jax.S...  68.2 us
    unnamed x11, local copies, waits for them, and re-layouts  5.12 us

profile of v3, /device:TPU:12, one launch (start us, length us, event | category | flops | bytes accessed | tf_op | source)
XLA Modules:
  0.0 73.3 jit_solution(10462141571076729255)
XLA Ops:
  0.0 0.0 copy-start
  0.0 1.2 %copy-done = f32[256,1024]{1,0:T(8,128)S(1)} copy-done((f32[256,1024]{1,0:T(8,128)S(1)}, f32[256,1024]{1,0:T(8,128)}, u32[]{:S(2)}) %copy-start) | copy-done | bytes 1048600
  1.2 0.0 copy-start.1
  1.2 0.8 %copy-done.1 = s32[3,2048]{1,0:T(4,128)S(1)} copy-done((s32[3,2048]{1,0:T(4,128)S(1)}, s32[3,2048]{1,0:T(4,128)}, u32[]{:S(2)}) %copy-start.1) | copy-done | bytes 24600
  2.0 0.0 copy-start.2
  2.0 0.8 %copy-done.2 = s32[3,2048]{1,0:T(4,128)S(1)} copy-done((s32[3,2048]{1,0:T(4,128)S(1)}, s32[3,2048]{1,0:T(4,128)}, u32[]{:S(2)}) %copy-start.2) | copy-done | bytes 24600
  2.7 0.0 copy-start.3
  2.7 0.8 %copy-done.3 = s32[3,2048]{1,0:T(4,128)S(1)} copy-done((s32[3,2048]{1,0:T(4,128)S(1)}, s32[3,2048]{1,0:T(4,128)}, u32[]{:S(2)}) %copy-start.3) | copy-done | bytes 24600
  3.5 0.0 copy-start.4
  3.5 0.7 copy-done.4
  4.2 68.2 %shard_map.55 = f32[256,1024]{1,0:T(8,128)S(1)} custom-call(f32[256,1024]{1,0:T(8,128)S(1)} %copy-done, s32[3,2048]{1,0:T(4,128)S(1)} %copy-done.1, s32[3,2048]{1,0:T(4,128)S(1)} %copy-done.2, s32[3,2048]{1,0:T(4,128)S(1)} %copy-done.3, s32[7]{0:T(128)S(1)} %copy-done.4), custom_call_target="tpu_custom_call" | custom-call | tf_op jit(solution)/shard_map/pallas_call | solution.py:591
  72.4 1.0 %copy.7 = f32[256,1024]{1,0:T(8,128)} copy(f32[256,1024]{1,0:T(8,128)S(1)} %shard_map.55) | data formatting | bytes 2097152
Async XLA Ops:
  0.0 1.2 %copy-start = (f32[256,1024]{1,0:T(8,128)S(1)}, f32[256,1024]{1,0:T(8,128)}, u32[]{:S(2)}) copy-start(f32[256,1024]{1,0:T(8,128)} %x_ref.1) | copy-start | bytes 3145732
  1.2 0.8 %copy-start.1 = (s32[3,2048]{1,0:T(4,128)S(1)}, s32[3,2048]{1,0:T(4,128)}, u32[]{:S(2)}) copy-start(s32[3,2048]{1,0:T(4,128)} %lower.1) | copy-start | bytes 73732
  2.0 0.8 %copy-start.2 = (s32[3,2048]{1,0:T(4,128)S(1)}, s32[3,2048]{1,0:T(4,128)}, u32[]{:S(2)}) copy-start(s32[3,2048]{1,0:T(4,128)} %upper.1) | copy-start | bytes 73732
  2.7 0.8 %copy-start.3 = (s32[3,2048]{1,0:T(4,128)S(1)}, s32[3,2048]{1,0:T(4,128)}, u32[]{:S(2)}) copy-start(s32[3,2048]{1,0:T(4,128)} %delays.1) | copy-start | bytes 73732
  3.5 0.7 copy-start.4

commit v4 on v3

--- a/solution.py
+++ b/solution.py
@@ -15,13 +15,16 @@
 UNROLL = 16
 CHUNKS_0 = 4
 CHUNK_ROWS = 16
+HEAD = 4
 HALO_LAG = 2
-MERGE_LAG = 3
-OWN_GROUP = 4
-OUTER_GROUP = 4
-NEAR_GROUP = 2
+OWN_GROUP = 2
 PLAN_UNROLL = 8
-EDGE_LAG = 4
+EDGE_LAG = 3
+REST_FIRST = 20
+REST_STEP = 3
+OWN_LEAD = 2
+COARSE = 64
+FINE = 8
 
 
 def shifted_2(block, axis, distance):
@@ -82,10 +85,10 @@
 
 
 def kernel(
-    tiles, tm_size, x_ref, lower, upper, delays, counts,
-    out_ref, columns, columns_0, places, plan_v, plan, picks_v, picks, raw, mine, cur, own_in, far_in, far_pass, halo_in, halo_pass,
+    tiles, tm_size, x_in, lower_in, upper_in, delays_in, counts_in,
+    out_ref, x_ref, lower, upper, delays, counts, columns, columns_0, places, plan_v, plan, picks_v, picks, raw, rim_in, mine, cur, own_in, far_in, far_pass, halo_in, halo_pass,
     picked, land, early, joined, final,
-    sent, s_plan, s_raw, s_far, s_far_pass, s_own, s_halo, s_halo_pass, s_fo, s_no, s_fi, s_edge,
+    sent, s_load, s_plan, s_raw, s_head, s_far, s_far_pass, s_own, s_halo, s_halo_pass, s_fo, s_last, s_edge,
 ):
     f, t = lax.axis_index("freq"), lax.axis_index("tm")
     c, z = lax.rem(f, 2), lax.div(f, 2)
@@ -104,6 +107,18 @@
     outer = zb == half
     has_later, has_earlier = t < tm_size - 1, t > 0
 
+    n0, chunk0 = CHUNKS_0, rows // CHUNKS_0
+
+    def load(j, source, target):
+        return pltpu.make_async_copy(source, target, s_load.at[j])
+
+    parts = [pl.ds(j * chunk0, chunk0) for j in range(n0)]
+    loads = [load(j, x_in.at[part], x_ref.at[part]) for j, part in enumerate(parts)]
+    pairs = ((lower_in, lower), (upper_in, upper), (delays_in, delays), (counts_in, counts))
+    table_loads = [load(n0 + j, *pair) for j, pair in enumerate(pairs)]
+    for copy in loads + table_loads:
+        copy.start()
+
     barrier = pltpu.get_barrier_semaphore()
 
     def greet(target):
@@ -129,6 +144,14 @@
 
     def span(j, group=1):
         return pl.ds(pl.multiple_of(j * chunk * group, chunk * group), chunk * group)
+
+    n_fine = rows // FINE
+
+    def coarse(j):
+        return pl.ds(pl.multiple_of(j * COARSE, COARSE), COARSE)
+
+    def fine(j):
+        return pl.ds(pl.multiple_of(j * FINE, FINE), FINE)
 
     def delayed(source, row, d, first):
         q, r = d >> 7, d & (LANES - 1)
@@ -138,34 +161,36 @@
         return jnp.where(lane >= r, a, b)
 
     def blocks(start, count, value, store):
-        def body(step, carry):
-            base = start + step * UNROLL
-            values = [(base + u, value(base, u)) for u in range(UNROLL)]
+        def body(base, size):
+            values = [(base + u, value(base, u)) for u in range(size)]
             for m, v in values:
                 store(m, v)
+
+        def step(i, carry):
+            body(start + i * UNROLL, UNROLL)
             return carry
 
-        if count == UNROLL:
-            body(0, 0)
+        if count <= UNROLL:
+            body(start, count)
         else:
-            lax.fori_loop(0, count // UNROLL, body, 0)
+            lax.fori_loop(0, count // UNROLL, step, 0)
 
     rim0 = rows // LANES
-    n0, chunk0 = CHUNKS_0, rows // CHUNKS_0
-
-    def raw_copy(kind, j, row, target, source_at, target_at, size):
-        span0 = pl.ds(row + j * chunk0, chunk0)
-        return remote(
-            raw.at[span0, pl.ds(source_at, size)], raw.at[span0, pl.ds(target_at, size)],
-            kind, s_raw.at[kind * n0 + j], target,
-        )
-
-    tail0 = (2 * tiles - rim0, tiles - rim0, rim0)
-    kept0 = (tiles - rim0, tiles - rim0, rim0)
-    full0 = (tiles, tiles, tiles)
-    own0 = lambda j, row: raw_copy(0, j, row, partner, *full0)
-    rim_out0 = lambda j: raw_copy(1, j, rows, later, *tail0)
-    rim_in0 = lambda j: raw_copy(2, j, rows, partner, *kept0)
+    full0, tail0, kept0 = pl.ds(tiles, tiles), pl.ds(2 * tiles - rim0, rim0), pl.ds(tiles - rim0, rim0)
+
+    def part_of(j, row=0):
+        return pl.ds(row, rows) if j is None else pl.ds(row + j * chunk0, chunk0)
+
+    def own0(j, row):
+        at_rows = raw.at[part_of(j, row), full0]
+        return remote(at_rows, at_rows, 0, s_raw.at[j or 0], partner)
+
+    def rim_out0(j):
+        return remote(raw.at[part_of(j, rows), tail0], rim_in.at[part_of(j), kept0], 1, s_raw.at[n0 + (j or 0)], later)
+
+    def rim_in0(j):
+        at_rows = rim_in.at[part_of(j), kept0]
+        return remote(at_rows, at_rows, 2, s_raw.at[2 * n0 + (j or 0)], partner)
 
     def spread(first, count):
         def body(step, carry):
@@ -178,8 +203,10 @@
 
         lax.fori_loop(0, count // SUBLANES, body, 0)
 
-    with phase("spread"):
-        spread(0, rows)
+    for j in range(n0):
+        with phase("spread"):
+            loads[j].wait()
+            spread(j * chunk0, chunk0)
     one = lambda cond: jnp.where(cond, 1, 0)
     with phase("greet"):
         pl.semaphore_wait(barrier, 3 + one(inner) + one(has_earlier) + one(has_later))
@@ -340,23 +367,30 @@
         pltpu.make_async_copy(picks_v, picks, s_plan.at[1]).start()
 
     with phase("order"):
+        for copy in table_loads:
+            copy.wait()
         find_order()
 
-    for j in range(n0):
-
-        @pl.when((c == 1) & has_earlier)
+    def take_rim():
+        for j in range(n0):
+
+            @pl.when((c == 1) & has_earlier)
+            def _():
+                with phase("rim_out"):
+                    rim_out0(j).wait_recv()
+                    rim_in0(j).start()
+
+        for j in range(n0):
+            with phase("rim_in"):
+                when((c == 0) & has_earlier, rim_in0(j).wait_recv)
+
+        @pl.when(has_earlier)
         def _():
-            with phase("rim_out"):
-                rim_out0(j).wait_recv()
-                rim_in0(j).start()
-
-    for j in range(n0):
-        with phase("own0"):
-            own0(j, (1 - c) * rows).wait_recv()
-        with phase("rim_in"):
-            when((c == 0) & has_earlier, rim_in0(j).wait_recv)
-
-    pltpu.make_async_copy(plan_v, plan, s_plan.at[0]).wait()
+            def fill(i):
+                raw[rows + i, :tiles, :] = rim_in[i]
+
+            clear(rows, fill)
+
     own_base, far_base = zb * 2 * rows, (1 - zb) * 2 * rows
     up_base = 2 * rows
     def entry(table, first, base, u):
@@ -368,9 +402,20 @@
         total = raw[lo, tiles:, :] + delayed(raw, up, d, tiles - rim0)
         return jnp.where((word >> 28) == 1, total, zero)
 
+    split = tiles // 2
+
     def store0(m, v):
         mine[m] = v
         cur[own_base + c * rows + m, tiles:, :] = v
+
+    def store_mine(m, v):
+        mine[m] = v
+
+    def store_head(m, v):
+        mine[m, split:, :] = v[split:, :]
+
+    def store_tail(m, v):
+        mine[m, :split, :] = v[:split, :]
 
     rim1 = 2 * rows // LANES
 
@@ -404,38 +449,49 @@
     def store2(m, v):
         final[m] = v
 
-    def finish(k):
-        start = pl.multiple_of(k * chunk, chunk)
-        for u in range(chunk):
-            join(start + u)
-        blocks(start, chunk, value2, store2)
-        for step in range(chunk // SUBLANES):
-            r = pl.multiple_of(start + step * SUBLANES, SUBLANES)
+    def finish(first, count):
+        def step(i, carry):
+            start = pl.multiple_of(first + i * FINE, FINE)
+            for u in range(FINE):
+                join(start + u)
+            blocks(start, FINE, value2, store2)
             for tile in range(tiles):
-                out_ref[pl.ds(r, SUBLANES), pl.ds(tile * LANES, LANES)] = final[pl.ds(r, SUBLANES), tile, :]
+                at_tile = pl.ds(tile * LANES, LANES)
+                out_ref[pl.ds(start, FINE), at_tile] = final[pl.ds(start, FINE), tile, :]
+            return carry
+
+        lax.fori_loop(0, count // FINE, step, 0)
 
     rim = pl.ds(tiles - rim1, rim1)
     every = pl.ds(0, rows)
 
     def flow(index, src, dst, sems, target):
-        def copy(j, group=1, sem=None):
+        def copy(j, group=1):
             at_rows = span(j, group)
-            return remote(src(at_rows), dst(at_rows), index, sems.at[j if sem is None else sem], target)
+            return remote(src(at_rows), dst(at_rows), index, sems.at[j], target)
+
+        copy.coarse = lambda j: remote(src(coarse(j)), dst(coarse(j)), index, sems.at[j], target)
+        copy.fine = lambda j: remote(src(fine(j)), dst(fine(j)), index, sems.at[lax.div(j, n_fine // sems.shape[0])], target)
 
         return copy, remote(src(every), dst(every), index, sems.at[0], target)
 
-    far, far_all = flow(3, lambda r: mine.at[r], lambda r: far_in.at[r], s_far, near)
+    lead, trail = pl.ds(split, tiles - split), pl.ds(0, split)
+    head, head_all = flow(3, lambda r: mine.at[r, lead], lambda r: far_in.at[r, lead], s_head, near)
+    far, far_all = flow(12, lambda r: mine.at[r, trail], lambda r: far_in.at[r, trail], s_far, near)
     far_on, far_on_all = flow(4, lambda r: far_in.at[r], lambda r: far_pass.at[r], s_far_pass, partner)
     own1, own1_all = flow(5, lambda r: mine.at[r], lambda r: own_in.at[r], s_own, partner)
     halo_mine, halo_all = flow(6, lambda r: mine.at[r, rim], lambda r: halo_in.at[r, rim], s_halo, later)
     halo_far, _ = flow(6, lambda r: far_in.at[r, rim], lambda r: halo_in.at[r, rim], s_halo, later)
     halo_on, halo_on_all = flow(7, lambda r: halo_in.at[r, rim], lambda r: halo_pass.at[r, rim], s_halo_pass, partner)
     to_half = lambda h: lambda r: land.at[h, r]
-    far_outer, far_outer_all = flow(8, lambda r: picked.at[0, r], to_half(half), s_fo, across)
-    near_outer, near_outer_all = flow(9, lambda r: picked.at[1, r], to_half(half), s_no, near)
-    far_inner, far_inner_all = flow(10, lambda r: picked.at[2, r], to_half(half), s_fi, facing)
+    _, far_outer_all = flow(8, lambda r: picked.at[0, r], to_half(half), s_fo, across)
+    far_outer = lambda j: remote(
+        picked.at[0, span(j)], land.at[half, span(j)], 8, s_fo.at[lax.div(j * chunk, COARSE)], across
+    )
+    near_outer, near_outer_all = flow(9, lambda r: picked.at[1, r], to_half(half), s_last, near)
+    far_inner, far_inner_all = flow(10, lambda r: picked.at[2, r], to_half(half), s_last, facing)
     got_across, _ = flow(8, lambda r: picked.at[0, r], to_half(1 - half), s_fo, across)
-    got_facing, _ = flow(10, lambda r: picked.at[2, r], to_half(1 - half), s_fi, facing)
+    got_facing, _ = flow(10, lambda r: picked.at[2, r], to_half(1 - half), s_last, facing)
     edge, edge_all = flow(11, lambda r: land.at[1, r], lambda r: early.at[r], s_edge, later)
 
     def loop(name, count, body):
@@ -446,44 +502,72 @@
 
         lax.fori_loop(0, count, step, 0)
 
-    def finish_lagged(j):
-        @pl.when(j >= EDGE_LAG)
+    last_rows = zb == 1
+    pieces = chunk // FINE
+    taken = (n_fine - 1 - REST_FIRST) // REST_STEP + 1
+
+    def take(j):
+        when(inner, got_facing.fine(j).wait_recv)
+        when(outer, near_outer.fine(j).wait_recv)
+        when(last_rows & has_later, edge.fine(j).start)
+
+    def keep_own(p):
+        blocks(p * chunk, chunk, value1(3), store_land)
+
+    def receive(p):
+        @pl.when(p < n)
         def _():
-            k = j - EDGE_LAG
+            for i in range(pieces):
+                j = p * pieces + i
+                when(outer | (half == 1) | (j >= taken), functools.partial(take, j))
+
+        when(inner & (half == 0) & (p < n - OWN_LEAD), functools.partial(keep_own, p + OWN_LEAD))
+
+        @pl.when(p >= EDGE_LAG)
+        def _():
+            k = p - EDGE_LAG
             when(has_earlier, edge(k).wait_recv)
-            finish(k)
+            finish(k * chunk, chunk)
+
+    when(inner, place_rows)
+    when(inner, pick_rows)
+    for j in range(n0):
+        with phase("own0"):
+            own0(j, (1 - c) * rows).wait_recv()
+    pltpu.make_async_copy(plan_v, plan, s_plan.at[0]).wait()
 
     @pl.when(outer)
     def _():
+        def send_head(j):
+            blocks(j * chunk, chunk, value0, store_head)
+            head(j).start()
+
+        loop("heads", HEAD, send_head)
+        take_rim()
+
         def produce(j):
-            blocks(j * chunk, chunk, value0, store0)
+            @pl.when(j < HEAD)
+            def _():
+                blocks(j * chunk, chunk, value0, store_tail)
+
             far(j).start()
 
+            @pl.when(j + HEAD < n)
+            def _():
+                blocks((j + HEAD) * chunk, chunk, value0, store_mine)
+                head(j + HEAD).start()
+
         loop("produce", n, produce)
 
         def from_across(j):
-            got_across(j, OUTER_GROUP).wait_recv()
-            for i in range(OUTER_GROUP):
-                when((half == 0) & has_later, edge(j * OUTER_GROUP + i).start)
-
-        loop("from_across", n // OUTER_GROUP, from_across)
-
-        def from_near(j):
-            @pl.when(j < n)
-            def _():
-                @pl.when(lax.rem(j, NEAR_GROUP) == 0)
-                def _():
-                    near_outer(lax.div(j, NEAR_GROUP), NEAR_GROUP).wait_recv()
-
-                when((half == 1) & has_later, edge(j).start)
-
-            finish_lagged(j)
-
-        loop("from_near", n + EDGE_LAG, from_near)
-
-        with phase("drain"):
-            far_all.wait_send()
-            when(has_later, edge_all.wait_send)
+            got_across.coarse(j).wait_recv()
+
+            @pl.when((half == 0) & has_later)
+            def _():
+                for i in range(COARSE // FINE):
+                    edge.fine(j * (COARSE // FINE) + i).start()
+
+        loop("from_across", rows // COARSE, from_across)
 
     @pl.when(inner)
     def _():
@@ -493,7 +577,24 @@
                 when((half == 0) & has_later, halo_mine(j * OWN_GROUP + i).start)
             own1(j, OWN_GROUP).start()
 
-        loop("produce", n // OWN_GROUP, produce)
+        take_rim()
+
+        def pass_head(j):
+            head(j).wait_recv()
+            when((half == 1) & has_later, halo_far(j).start)
+
+        def pass_halo(j):
+            @pl.when(has_earlier)
+            def _():
+                halo_mine(j).wait_recv()
+                halo_on(j).start()
+
+        first_rows = functools.partial(loop, "produce", HEAD // OWN_GROUP, produce)
+        when(half == 0, first_rows)
+        loop("heads", HEAD, pass_head)
+        when(half == 1, first_rows)
+        pltpu.make_async_copy(picks_v, picks, s_plan.at[1]).wait()
+        loop("halos", HEAD - HALO_LAG, pass_halo)
 
         def gather(k):
             @pl.when(lax.rem(k, OWN_GROUP) == 0)
@@ -516,70 +617,64 @@
                     cur[up_base + other_at + u, :tiles, :] = halo_pass[start + u]
 
             blocks(k * chunk, chunk, value1(0), store_picked(0))
-            far_outer(k, 1, lax.div(k, OUTER_GROUP)).start()
+            far_outer(k).start()
 
         def stream(j):
+            when(j > 0, functools.partial(gather, j - 1))
+
             @pl.when(j < n)
             def _():
                 far(j).wait_recv()
                 far_on(j).start()
-                when((half == 1) & has_later, halo_far(j).start)
-
-            pl.when(j == 0)(place_rows)
-            pl.when(j == 1)(pick_rows)
-
-            @pl.when((j >= HALO_LAG) & (j < n + HALO_LAG) & has_earlier)
-            def _():
-                halo_mine(j - HALO_LAG).wait_recv()
-                halo_on(j - HALO_LAG).start()
-
-            when(j == MERGE_LAG, pltpu.make_async_copy(picks_v, picks, s_plan.at[1]).wait)
-
-            @pl.when(j >= MERGE_LAG)
-            def _():
-                gather(j - MERGE_LAG)
-
-        loop("stream", n + MERGE_LAG, stream)
+
+            when(j < n - HEAD, functools.partial(pass_head, j + HEAD))
+            when(j < n - HEAD + HALO_LAG, functools.partial(pass_halo, j + HEAD - HALO_LAG))
+            group = lax.div(j + HEAD, OWN_GROUP)
+            when((lax.rem(j, OWN_GROUP) == 0) & (group < n // OWN_GROUP), functools.partial(produce, group))
+
+        loop("stream", n + 1, stream)
 
         def rest(j):
-            for i in range(NEAR_GROUP):
-                k = j * NEAR_GROUP + i
-                blocks(k * chunk, chunk, value1(2), store_picked(2))
-                far_inner(k).start()
-                blocks(k * chunk, chunk, value1(1), store_picked(1))
-                blocks(k * chunk, chunk, value1(3), store_land)
-                when((half == 1) & has_later, edge(k).start)
-            near_outer(j, NEAR_GROUP).start()
-
-        loop("rest", n // NEAR_GROUP, rest)
-
-        def receive(j):
-            @pl.when(j < n)
-            def _():
-                got_facing(j).wait_recv()
-                when((half == 0) & has_later, edge(j).start)
-
-            finish_lagged(j)
-
-        loop("receive", n + EDGE_LAG, receive)
-
-        with phase("drain"):
-            own1_all.wait_send()
-            far_on_all.wait_send()
-            when(has_later, halo_all.wait_send)
-            when(has_earlier, halo_on_all.wait_send)
-            far_outer_all.wait_send()
-            near_outer_all.wait_send()
-            far_inner_all.wait_send()
-            when(has_later, edge_all.wait_send)
-
-    raw_all = lambda kind, row, target, source_at, target_at, size: remote(
-        raw.at[pl.ds(row, rows), pl.ds(source_at, size)], raw.at[pl.ds(row, rows), pl.ds(target_at, size)],
-        kind, s_raw.at[0], target,
-    )
-    raw_all(0, c * rows, partner, *full0).wait_send()
-    when((c == 1) & has_later, raw_all(1, rows, later, *tail0).wait_send)
-    when((c == 1) & has_earlier, raw_all(2, rows, partner, *kept0).wait_send)
+            blocks(j * FINE, FINE, value1(2), store_picked(2))
+            far_inner.fine(j).start()
+            blocks(j * FINE, FINE, value1(1), store_picked(1))
+            near_outer.fine(j).start()
+
+            @pl.when(half == 1)
+            def _():
+                blocks(j * FINE, FINE, value1(3), store_land)
+                when(has_later, edge.fine(j).start)
+
+            turn = j - REST_FIRST
+
+            @pl.when((half == 0) & (turn >= 0) & (lax.rem(jnp.maximum(turn, 0), REST_STEP) == 0))
+            def _():
+                take(lax.div(turn, REST_STEP))
+
+        loop("rest", n_fine, rest)
+        when(half == 0, functools.partial(loop, "own", OWN_LEAD, keep_own))
+
+    loop("receive", n + EDGE_LAG, receive)
+
+    @pl.when(outer)
+    def _():
+        head_all.wait_send()
+        far_all.wait_send()
+
+    @pl.when(inner)
+    def _():
+        own1_all.wait_send()
+        far_on_all.wait_send()
+        when(has_later, halo_all.wait_send)
+        when(has_earlier, halo_on_all.wait_send)
+        far_outer_all.wait_send()
+        near_outer_all.wait_send()
+        far_inner_all.wait_send()
+
+    when(has_later, edge_all.wait_send)
+    own0(None, c * rows).wait_send()
+    when((c == 1) & has_later, rim_out0(None).wait_send)
+    when((c == 1) & has_earlier, rim_in0(None).wait_send)
 
 
 def per_device_fused(tm_size, band_state, lower_rows, upper_rows, delays, counts):
@@ -590,10 +685,15 @@
     wide = pltpu.VMEM((row_count, tiles, LANES), jnp.float32)
     return pl.pallas_call(
         functools.partial(kernel, tiles, tm_size),
-        out_shape=jax.ShapeDtypeStruct((row_count, samples), jnp.float32),
-        in_specs=[pl.BlockSpec(memory_space=pltpu.VMEM)] * 4 + [pl.BlockSpec(memory_space=pltpu.SMEM)],
+        out_shape=pltpu.VMEM((row_count, samples), jnp.float32),
+        in_specs=[pl.BlockSpec(memory_space=pltpu.HBM)] * 5,
         out_specs=pl.BlockSpec(memory_space=pltpu.VMEM),
         scratch_shapes=[
+            pltpu.VMEM(band_state.shape, jnp.float32),
+            pltpu.VMEM(lower_rows.shape, jnp.int32),
+            pltpu.VMEM(upper_rows.shape, jnp.int32),
+            pltpu.VMEM(delays.shape, jnp.int32),
+            pltpu.SMEM(counts.shape, jnp.int32),
             pltpu.VMEM((4 * row_count, LANES), jnp.int32),
             pltpu.VMEM((2 * row_count, LANES), jnp.int32),
             pltpu.VMEM((2 * row_count, LANES), jnp.int32),
@@ -603,6 +703,7 @@
             pltpu.SMEM((4 * row_count // LANES, LANES), jnp.int32),
             pltpu.VMEM((2 * row_count, 2 * tiles, LANES), jnp.float32),
             wide,
+            wide,
             pltpu.VMEM((4 * row_count, 2 * tiles, LANES), jnp.float32),
             wide, wide, wide, wide, wide,
             pltpu.VMEM((3, row_count, tiles, LANES), jnp.float32),
@@ -610,21 +711,22 @@
             wide,
             pltpu.VMEM((row_count, 2 * tiles, LANES), jnp.float32),
             wide,
-            dma((12,)),
+            dma((13,)),
+            dma((CHUNKS_0 + 4,)),
             dma((2,)),
             dma((3 * CHUNKS_0,)),
+            dma((n,)),
             dma((n,)),
             dma((n,)),
             dma((n // OWN_GROUP,)),
             dma((n,)),
             dma((n,)),
-            dma((n // OUTER_GROUP,)),
-            dma((n // NEAR_GROUP,)),
-            dma((n,)),
+            dma((row_count // COARSE,)),
+            dma((row_count // FINE,)),
             dma((n,)),
         ],
         compiler_params=pltpu.CompilerParams(
-            collective_id=0, has_side_effects=True, vmem_limit_bytes=36 * 2**20
+            collective_id=0, has_side_effects=True, vmem_limit_bytes=58 * 2**20
         ),
     )(band_state, lower_rows, upper_rows, delays, counts)
 

time: 73.8 us -> 67.4 us (0.913)
  local copies, waits for them, and re-layouts: 5.12 us -> 0.97 us
  Pallas kernels: 68.2 us -> 66.2 us
    unnamed x11 -> x1, local copies, waits for them, and re-layouts: 5.12 us -> 0.97 us
    pallas_call x1, Pallas kernels: 68.2 us -> 66.2 us  [per_device_fused(): pl.pallas_call(functools.partial(kernel, tiles, tm_size), out_shape=pltpu...]
where the time goes in v4:
time: 67.4 us; the launch traced here: 67.2 us
  Pallas kernels  66.2 us (98%)
  local copies, waits for them, and re-layouts  0.97 us (1%)
    pallas_call x1, Pallas kernels, per_device_fused(): pl.pallas_call(functools.partial(kernel, tiles, tm_size), out_shape=pltpu...  66.2 us

profile of v4, /device:TPU:12, one launch (start us, length us, event | category | flops | bytes accessed | tf_op | source)
XLA Modules:
  0.0 67.2 jit_solution(10969913153696476178)
XLA Ops:
  0.0 66.2 %shard_map.55 = f32[256,1024]{1,0:T(8,128)S(1)} custom-call(f32[256,1024]{1,0:T(8,128)} %x_in.1, s32[3,2048]{1,0:T(4,128)} %lower_in.1, s32[3,2048]{1,0:T(4,128)} %upper_in.1, s32[3,2048]{1,0:T(4,128)} %delays_in.1, s32[7]{0:T(128)} %counts_in.1), custom_call_target="tpu_custom_call" | custom-call | tf_op jit(solution)/shard_map/pallas_call | solution.py:686
  66.2 1.0 %copy.7 = f32[256,1024]{1,0:T(8,128)} copy(f32[256,1024]{1,0:T(8,128)S(1)} %shard_map.55) | data formatting | bytes 2097152

commit v5 on v4

--- a/solution.py
+++ b/solution.py
@@ -13,18 +13,19 @@
 LANES = 128
 SUBLANES = 8
 UNROLL = 16
-CHUNKS_0 = 4
+CHUNKS_0 = 2
 CHUNK_ROWS = 16
-HEAD = 4
+HEAD = 2
 HALO_LAG = 2
+FIRST_OWN = 2
 OWN_GROUP = 2
 PLAN_UNROLL = 8
 EDGE_LAG = 3
-REST_FIRST = 20
-REST_STEP = 3
+REST_FIRST = 9
+REST_STEP = 2
 OWN_LEAD = 2
 COARSE = 64
-FINE = 8
+FINE = 16
 
 
 def shifted_2(block, axis, distance):
@@ -192,10 +193,10 @@
         at_rows = rim_in.at[part_of(j), kept0]
         return remote(at_rows, at_rows, 2, s_raw.at[2 * n0 + (j or 0)], partner)
 
-    def spread(first, count):
+    def spread(first, count, first_tile, last_tile):
         def body(step, carry):
             r = first + step * SUBLANES
-            for tile in range(tiles):
+            for tile in range(first_tile, last_tile):
                 raw[pl.ds(c * rows + r, SUBLANES), tiles + tile, :] = x_ref[
                     pl.ds(r, SUBLANES), pl.ds(tile * LANES, LANES)
                 ]
@@ -206,13 +207,15 @@
     for j in range(n0):
         with phase("spread"):
             loads[j].wait()
-            spread(j * chunk0, chunk0)
+            spread(j * chunk0, chunk0, tiles - rim0, tiles)
     one = lambda cond: jnp.where(cond, 1, 0)
     with phase("greet"):
         pl.semaphore_wait(barrier, 3 + one(inner) + one(has_earlier) + one(has_later))
-    with phase("send0"):
-        for j in range(n0):
-            when((c == 1) & has_later, rim_out0(j).start)
+    for j in range(n0):
+        when((c == 1) & has_later, rim_out0(j).start)
+    for j in range(n0):
+        with phase("send0"):
+            spread(j * chunk0, chunk0, 0, tiles - rim0)
             own0(j, c * rows).start()
 
     def clear(count, store):
@@ -589,10 +592,12 @@
                 halo_mine(j).wait_recv()
                 halo_on(j).start()
 
-        first_rows = functools.partial(loop, "produce", HEAD // OWN_GROUP, produce)
-        when(half == 0, first_rows)
-        loop("heads", HEAD, pass_head)
-        when(half == 1, first_rows)
+        def begin(j):
+            when(half == 1, functools.partial(pass_head, j))
+            produce(j)
+
+        loop("produce", FIRST_OWN, begin)
+        loop("heads", HEAD, lambda j: when((half == 0) | (j >= FIRST_OWN), functools.partial(pass_head, j)))
         pltpu.make_async_copy(picks_v, picks, s_plan.at[1]).wait()
         loop("halos", HEAD - HALO_LAG, pass_halo)
 
@@ -627,9 +632,9 @@
                 far(j).wait_recv()
                 far_on(j).start()
 
+            when(j < n - HEAD + HALO_LAG, functools.partial(pass_halo, j + HEAD - HALO_LAG))
             when(j < n - HEAD, functools.partial(pass_head, j + HEAD))
-            when(j < n - HEAD + HALO_LAG, functools.partial(pass_halo, j + HEAD - HALO_LAG))
-            group = lax.div(j + HEAD, OWN_GROUP)
+            group = lax.div(j, OWN_GROUP) + FIRST_OWN
             when((lax.rem(j, OWN_GROUP) == 0) & (group < n // OWN_GROUP), functools.partial(produce, group))
 
         loop("stream", n + 1, stream)

time: 67.4 us -> 66.6 us (0.988)
  Pallas kernels: 66.2 us -> 65.5 us
    pallas_call x1, Pallas kernels: 66.2 us -> 65.5 us  [per_device_fused(): pl.pallas_call(functools.partial(kernel, tiles, tm_size), out_shape=pltpu...]
where the time goes in v5:
time: 66.6 us; the launch traced here: 66.5 us
  Pallas kernels  65.5 us (98%)
  local copies, waits for them, and re-layouts  0.97 us (1%)
    pallas_call x1, Pallas kernels, per_device_fused(): pl.pallas_call(functools.partial(kernel, tiles, tm_size), out_shape=pltpu...  65.5 us

profile of v5, /device:TPU:12, one launch (start us, length us, event | category | flops | bytes accessed | tf_op | source)
XLA Modules:
  0.0 66.5 jit_solution(6701269946762312309)
XLA Ops:
  0.0 65.5 %shard_map.55 = f32[256,1024]{1,0:T(8,128)S(1)} custom-call(f32[256,1024]{1,0:T(8,128)} %x_in.1, s32[3,2048]{1,0:T(4,128)} %lower_in.1, s32[3,2048]{1,0:T(4,128)} %upper_in.1, s32[3,2048]{1,0:T(4,128)} %delays_in.1, s32[7]{0:T(128)} %counts_in.1), custom_call_target="tpu_custom_call" | custom-call | tf_op jit(solution)/shard_map/pallas_call | solution.py:691
  65.5 1.0 %copy.7 = f32[256,1024]{1,0:T(8,128)} copy(f32[256,1024]{1,0:T(8,128)S(1)} %shard_map.55) | data formatting | bytes 2097152

commit v6 on v5

--- a/solution.py
+++ b/solution.py
@@ -24,6 +24,7 @@
 REST_FIRST = 9
 REST_STEP = 2
 OWN_LEAD = 2
+CROSS = 2
 COARSE = 64
 FINE = 16
 
@@ -88,8 +89,8 @@
 def kernel(
     tiles, tm_size, x_in, lower_in, upper_in, delays_in, counts_in,
     out_ref, x_ref, lower, upper, delays, counts, columns, columns_0, places, plan_v, plan, picks_v, picks, raw, rim_in, mine, cur, own_in, far_in, far_pass, halo_in, halo_pass,
-    picked, land, early, joined, final,
-    sent, s_load, s_plan, s_raw, s_head, s_far, s_far_pass, s_own, s_halo, s_halo_pass, s_fo, s_last, s_edge,
+    picked, land, early, cross_own, cross_in, joined, final,
+    sent, s_load, s_plan, s_raw, s_head, s_far, s_far_pass, s_own, s_halo, s_halo_pass, s_fo, s_last, s_edge, s_cross,
 ):
     f, t = lax.axis_index("freq"), lax.axis_index("tm")
     c, z = lax.rem(f, 2), lax.div(f, 2)
@@ -241,6 +242,11 @@
         clear(2 * rows, clear_cur)
         clear(rows, clear_early)
 
+        def clear_cross(i):
+            cross_in[i] = zero
+
+        clear(CROSS * CHUNK_ROWS, clear_cross)
+
     chip_rows, half_rows = 2 * rows, 4 * rows
     flat = (SUBLANES, LANES)
     lane_at = lax.broadcasted_iota(jnp.int32, flat, 1)
@@ -335,6 +341,8 @@
             start = f * rows + g * LANES
             live = bit(lane_at + start < counts[2**ITERS - 2], 12)
             plan_v[pl.ds(rows // LANES + g, 1), :] = (row_of(delays, 2, start) | live)[0:1]
+        facing_end = (f + 2 - 4 * half) * rows + rows - LANES
+        plan_v[pl.ds(2 * rows // LANES, 1), :] = row_of(delays, 2, facing_end)[0:1]
         pltpu.make_async_copy(plan_v, plan, s_plan.at[0]).start()
 
     def place_rows():
@@ -452,12 +460,13 @@
     def store2(m, v):
         final[m] = v
 
-    def finish(first, count):
+    def finish(first, count, prepare, value):
         def step(i, carry):
             start = pl.multiple_of(first + i * FINE, FINE)
-            for u in range(FINE):
-                join(start + u)
-            blocks(start, FINE, value2, store2)
+            if prepare is not None:
+                for u in range(FINE):
+                    prepare(start + u)
+            blocks(start, FINE, value, store2)
             for tile in range(tiles):
                 at_tile = pl.ds(tile * LANES, LANES)
                 out_ref[pl.ds(start, FINE), at_tile] = final[pl.ds(start, FINE), tile, :]
@@ -509,10 +518,33 @@
     pieces = chunk // FINE
     taken = (n_fine - 1 - REST_FIRST) // REST_STEP + 1
 
+    n_plain = n - CROSS
+    cross_row = n_plain * chunk
+    joins_here = outer | (half == 1)
+    whole = pl.ds(0, CROSS * chunk)
+    cross = remote(cross_own.at[whole], cross_in.at[whole], 13, s_cross.at[0], later)
+
     def take(j):
         when(inner, got_facing.fine(j).wait_recv)
         when(outer, near_outer.fine(j).wait_recv)
-        when(last_rows & has_later, edge.fine(j).start)
+        when(last_rows & has_later & (joins_here | (j < n_plain * pieces)), edge.fine(j).start)
+
+    def store_cross(m, v):
+        cross_own[m - cross_row] = v
+
+    def cross_value(base, u):
+        word = entry(plan, rows // LANES + 1, base, u)
+        return delayed(joined, base + u, word, 0)
+
+    def plain_value(base, u):
+        word = entry(plan, rows // LANES, base, u)
+        return jnp.where((word >> 12) == 1, land[0, base + u] + land[1, base + u], zero)
+
+    def send_crossed(first):
+        for u in range(FINE):
+            joined[first + u, :tiles, :] = cross_in[first - cross_row + u]
+            joined[first + u, tiles:, :] = cross_own[first - cross_row + u]
+        blocks(first, FINE, cross_value, store_picked(2))
 
     def keep_own(p):
         blocks(p * chunk, chunk, value1(3), store_land)
@@ -529,8 +561,16 @@
         @pl.when(p >= EDGE_LAG)
         def _():
             k = p - EDGE_LAG
-            when(has_earlier, edge(k).wait_recv)
-            finish(k * chunk, chunk)
+            joins = joins_here | (k < n_plain)
+
+            @pl.when(joins)
+            def _():
+                when(has_earlier, edge(k).wait_recv)
+                finish(k * chunk, chunk, join, value2)
+
+            @pl.when(jnp.logical_not(joins))
+            def _():
+                finish(k * chunk, chunk, None, plain_value)
 
     when(inner, place_rows)
     when(inner, pick_rows)
@@ -639,8 +679,23 @@
 
         loop("stream", n + 1, stream)
 
+        @pl.when(half == 1)
+        def _():
+            blocks(cross_row, CROSS * chunk, value1(2), store_cross)
+            when(has_later, cross.start)
+
         def rest(j):
-            blocks(j * FINE, FINE, value1(2), store_picked(2))
+            crossed = (half == 1) & (j >= n_plain * pieces)
+
+            @pl.when(crossed)
+            def _():
+                when(has_earlier & (j == n_plain * pieces), cross.wait_recv)
+                send_crossed(pl.multiple_of(j * FINE, FINE))
+
+            @pl.when(jnp.logical_not(crossed))
+            def _():
+                blocks(j * FINE, FINE, value1(2), store_picked(2))
+
             far_inner.fine(j).start()
             blocks(j * FINE, FINE, value1(1), store_picked(1))
             near_outer.fine(j).start()
@@ -676,7 +731,12 @@
         near_outer_all.wait_send()
         far_inner_all.wait_send()
 
-    when(has_later, edge_all.wait_send)
+        when((half == 1) & has_later, cross.wait_send)
+
+    plain = pl.ds(0, cross_row)
+    edge_plain = remote(land.at[1, plain], early.at[plain], 11, s_edge.at[0], later)
+    when(has_later & joins_here, edge_all.wait_send)
+    when(has_later & jnp.logical_not(joins_here), edge_plain.wait_send)
     own0(None, c * rows).wait_send()
     when((c == 1) & has_later, rim_out0(None).wait_send)
     when((c == 1) & has_earlier, rim_in0(None).wait_send)
@@ -702,8 +762,8 @@
             pltpu.VMEM((4 * row_count, LANES), jnp.int32),
             pltpu.VMEM((2 * row_count, LANES), jnp.int32),
             pltpu.VMEM((2 * row_count, LANES), jnp.int32),
-            pltpu.VMEM((2 * row_count // LANES, LANES), jnp.int32),
-            pltpu.SMEM((2 * row_count // LANES, LANES), jnp.int32),
+            pltpu.VMEM((4 * row_count // LANES, LANES), jnp.int32),
+            pltpu.SMEM((4 * row_count // LANES, LANES), jnp.int32),
             pltpu.VMEM((4 * row_count // LANES, LANES), jnp.int32),
             pltpu.SMEM((4 * row_count // LANES, LANES), jnp.int32),
             pltpu.VMEM((2 * row_count, 2 * tiles, LANES), jnp.float32),
@@ -714,9 +774,11 @@
             pltpu.VMEM((3, row_count, tiles, LANES), jnp.float32),
             pltpu.VMEM((2, row_count, tiles, LANES), jnp.float32),
             wide,
+            pltpu.VMEM((CROSS * CHUNK_ROWS, tiles, LANES), jnp.float32),
+            pltpu.VMEM((CROSS * CHUNK_ROWS, tiles, LANES), jnp.float32),
             pltpu.VMEM((row_count, 2 * tiles, LANES), jnp.float32),
             wide,
-            dma((13,)),
+            dma((14,)),
             dma((CHUNKS_0 + 4,)),
             dma((2,)),
             dma((3 * CHUNKS_0,)),
@@ -729,6 +791,7 @@
             dma((row_count // COARSE,)),
             dma((row_count // FINE,)),
             dma((n,)),
+            dma((1,)),
         ],
         compiler_params=pltpu.CompilerParams(
             collective_id=0, has_side_effects=True, vmem_limit_bytes=58 * 2**20

time: 66.6 us -> 65.4 us (0.982)
  the two profiles are of different devices: /device:TPU:12 before, /device:TPU:5 now
where the time goes in v6:
time: 65.4 us; the launch traced here: 65.3 us
  Pallas kernels  64.3 us (98%)
  local copies, waits for them, and re-layouts  0.97 us (1%)
    pallas_call x1, Pallas kernels, per_device_fused(): pl.pallas_call(functools.partial(kernel, tiles, tm_size), out_shape=pltpu...  64.3 us

profile of v6, /device:TPU:5, one launch (start us, length us, event | category | flops | bytes accessed | tf_op | source)
XLA Modules:
  0.0 65.3 jit_solution(12261757993171438285)
XLA Ops:
  0.0 64.3 %shard_map.55 = f32[256,1024]{1,0:T(8,128)S(1)} custom-call(f32[256,1024]{1,0:T(8,128)} %x_in.1, s32[3,2048]{1,0:T(4,128)} %lower_in.1, s32[3,2048]{1,0:T(4,128)} %upper_in.1, s32[3,2048]{1,0:T(4,128)} %delays_in.1, s32[7]{0:T(128)} %counts_in.1), custom_call_target="tpu_custom_call" | custom-call | tf_op jit(solution)/shard_map/pallas_call | solution.py:751
  64.3 1.0 %copy.7 = f32[256,1024]{1,0:T(8,128)} copy(f32[256,1024]{1,0:T(8,128)S(1)} %shard_map.55) | data formatting | bytes 2097152

commit v7 on v6

--- a/solution.py
+++ b/solution.py
@@ -20,7 +20,7 @@
 FIRST_OWN = 2
 OWN_GROUP = 2
 PLAN_UNROLL = 8
-EDGE_LAG = 3
+EDGE_LAG = 2
 REST_FIRST = 9
 REST_STEP = 2
 OWN_LEAD = 2
@@ -558,9 +558,10 @@
 
         when(inner & (half == 0) & (p < n - OWN_LEAD), functools.partial(keep_own, p + OWN_LEAD))
 
-        @pl.when(p >= EDGE_LAG)
+        k = p - jnp.where(last_rows, EDGE_LAG, 0)
+
+        @pl.when((k >= 0) & (k < n))
         def _():
-            k = p - EDGE_LAG
             joins = joins_here | (k < n_plain)
 
             @pl.when(joins)

time: 65.4 us -> 64.8 us (level)
  the two profiles are of different devices: /device:TPU:5 before, /device:TPU:12 now
where the time goes in v7:
time: 64.8 us; the launch traced here: 64.1 us
  Pallas kernels  63.1 us (97%)
  local copies, waits for them, and re-layouts  0.97 us (1%)
    pallas_call x1, Pallas kernels, per_device_fused(): pl.pallas_call(functools.partial(kernel, tiles, tm_size), out_shape=pltpu...  63.1 us

profile of v7, /device:TPU:12, one launch (start us, length us, event | category | flops | bytes accessed | tf_op | source)
XLA Modules:
  0.0 64.1 jit_solution(16972756298431008884)
XLA Ops:
  0.0 63.1 %shard_map.55 = f32[256,1024]{1,0:T(8,128)S(1)} custom-call(f32[256,1024]{1,0:T(8,128)} %x_in.1, s32[3,2048]{1,0:T(4,128)} %lower_in.1, s32[3,2048]{1,0:T(4,128)} %upper_in.1, s32[3,2048]{1,0:T(4,128)} %delays_in.1, s32[7]{0:T(128)} %counts_in.1), custom_call_target="tpu_custom_call" | custom-call | tf_op jit(solution)/shard_map/pallas_call | solution.py:752
  63.2 1.0 %copy.7 = f32[256,1024]{1,0:T(8,128)} copy(f32[256,1024]{1,0:T(8,128)S(1)} %shard_map.55) | data formatting | bytes 2097152

commit v8 on v7

--- a/solution.py
+++ b/solution.py
@@ -227,26 +227,6 @@
 
         lax.fori_loop(0, count // UNROLL, body, 0)
 
-    @pl.when(t == 0)
-    def _():
-        def clear_raw(i):
-            raw[rows + i, :tiles, :] = zero
-
-        def clear_cur(i):
-            cur[2 * rows + i, :tiles, :] = zero
-
-        def clear_early(i):
-            early[i] = zero
-
-        clear(rows, clear_raw)
-        clear(2 * rows, clear_cur)
-        clear(rows, clear_early)
-
-        def clear_cross(i):
-            cross_in[i] = zero
-
-        clear(CROSS * CHUNK_ROWS, clear_cross)
-
     chip_rows, half_rows = 2 * rows, 4 * rows
     flat = (SUBLANES, LANES)
     lane_at = lax.broadcasted_iota(jnp.int32, flat, 1)
@@ -514,6 +494,26 @@
 
         lax.fori_loop(0, count, step, 0)
 
+    @pl.when(t == 0)
+    def _():
+        def clear_raw(i):
+            raw[rows + i, :tiles, :] = zero
+
+        def clear_cur(i):
+            cur[2 * rows + i, :tiles, :] = zero
+
+        def clear_early(i):
+            early[i] = zero
+
+        clear(rows, clear_raw)
+        when(inner, lambda: clear(2 * rows, clear_cur))
+        clear(rows, clear_early)
+
+        def clear_cross(i):
+            cross_in[i] = zero
+
+        clear(CROSS * CHUNK_ROWS, clear_cross)
+
     last_rows = zb == 1
     pieces = chunk // FINE
     taken = (n_fine - 1 - REST_FIRST) // REST_STEP + 1
@@ -686,6 +686,8 @@
             when(has_later, cross.start)
 
         def rest(j):
+            blocks(j * FINE, FINE, value1(1), store_picked(1))
+            near_outer.fine(j).start()
             crossed = (half == 1) & (j >= n_plain * pieces)
 
             @pl.when(crossed)
@@ -698,8 +700,6 @@
                 blocks(j * FINE, FINE, value1(2), store_picked(2))
 
             far_inner.fine(j).start()
-            blocks(j * FINE, FINE, value1(1), store_picked(1))
-            near_outer.fine(j).start()
 
             @pl.when(half == 1)
             def _():

time: 64.8 us -> 64.8 us (level)
  no operation moved by 1% of the time
where the time goes in v8:
time: 64.8 us; the launch traced here: 64 us
  Pallas kernels  63 us (97%)
  local copies, waits for them, and re-layouts  0.97 us (1%)
    pallas_call x1, Pallas kernels, per_device_fused(): pl.pallas_call(functools.partial(kernel, tiles, tm_size), out_shape=pltpu...  63 us

profile of v8, /device:TPU:12, one launch (start us, length us, event | category | flops | bytes accessed | tf_op | source)
XLA Modules:
  0.0 64.0 jit_solution(15782640890065793012)
XLA Ops:
  0.0 63.0 %shard_map.55 = f32[256,1024]{1,0:T(8,128)S(1)} custom-call(f32[256,1024]{1,0:T(8,128)} %x_in.1, s32[3,2048]{1,0:T(4,128)} %lower_in.1, s32[3,2048]{1,0:T(4,128)} %upper_in.1, s32[3,2048]{1,0:T(4,128)} %delays_in.1, s32[7]{0:T(128)} %counts_in.1), custom_call_target="tpu_custom_call" | custom-call | tf_op jit(solution)/shard_map/pallas_call | solution.py:752
  63.0 1.0 %copy.7 = f32[256,1024]{1,0:T(8,128)} copy(f32[256,1024]{1,0:T(8,128)S(1)} %shard_map.55) | data formatting | bytes 2097152

commit v9 on v7

--- a/solution.py
+++ b/solution.py
@@ -17,11 +17,11 @@
 CHUNK_ROWS = 16
 HEAD = 2
 HALO_LAG = 2
-FIRST_OWN = 2
+FIRST_OWN = 1
 OWN_GROUP = 2
 PLAN_UNROLL = 8
 EDGE_LAG = 2
-REST_FIRST = 9
+REST_FIRST = 8
 REST_STEP = 2
 OWN_LEAD = 2
 CROSS = 2

time: 64.8 us -> 64.8 us (level)
  no operation moved by 1% of the time
where the time goes in v9:
time: 64.8 us; the launch traced here: 64.4 us
  Pallas kernels  63.4 us (98%)
  local copies, waits for them, and re-layouts  0.97 us (1%)
    pallas_call x1, Pallas kernels, per_device_fused(): pl.pallas_call(functools.partial(kernel, tiles, tm_size), out_shape=pltpu...  63.4 us

profile of v9, /device:TPU:12, one launch (start us, length us, event | category | flops | bytes accessed | tf_op | source)
XLA Modules:
  0.0 64.4 jit_solution(12876566610792576635)
XLA Ops:
  0.0 63.4 %shard_map.55 = f32[256,1024]{1,0:T(8,128)S(1)} custom-call(f32[256,1024]{1,0:T(8,128)} %x_in.1, s32[3,2048]{1,0:T(4,128)} %lower_in.1, s32[3,2048]{1,0:T(4,128)} %upper_in.1, s32[3,2048]{1,0:T(4,128)} %delays_in.1, s32[7]{0:T(128)} %counts_in.1), custom_call_target="tpu_custom_call" | custom-call | tf_op jit(solution)/shard_map/pallas_call | solution.py:752
  63.4 1.0 %copy.7 = f32[256,1024]{1,0:T(8,128)} copy(f32[256,1024]{1,0:T(8,128)S(1)} %shard_map.55) | data formatting | bytes 2097152
